TPU v7x, 256 devices: a 4x2x16 block of a 4x16x16 slice. The times are simulated.
256 devices in a mesh: groups: 2 (over y), patch: 16 (over z), cfg: 2 (over core), head: 4 (over x).
Axes of the slice: x: 4, y: 2, z: 16, core: 2. Of those that a mesh axis runs over, the one named last changes fastest.
The devices are a block of a 4x16x16 slice.
Arguments:
- img_hidden: bfloat16 [2, 8192, 3072], P('cfg', ('groups', 'patch')), parts along dimension 1, may hold values from -40 to 40
- txt_hidden: bfloat16 [2, 512, 3072], P('cfg', ('groups', 'patch')), parts along dimension 1, may hold values from -6 to 6
- modulation: float32 [4, 3, 3072], P(('groups', 'cfg')), parts along dimension 0, may hold values from -4 to 4
- w_qkv: bfloat16 [3072, 3, 1536], P(None, None, 'head'), may hold values from -0.109375 to 0.109375
- q_gain: float32 [128], replicated, may hold values from 1.2 to 2.5
- k_gain: float32 [128], replicated, may hold values from 1.2 to 2.5
- w_out: bfloat16 [1536, 3072], P('head'), may hold values from -0.15625 to 0.15625
- b_out: float32 [3072], replicated, may hold values from -3 to 3
- stale_kv: bfloat16 [2, 2, 8704, 1536], P('cfg', None, ('groups', 'patch'), 'head'), parts along dimension 2, may hold values from -500 to 500
- final_mod: float32 [4, 2, 3072], P(('groups', 'cfg')), parts along dimension 0, may hold values from -3 to 3
- w_final: bfloat16 [3072, 64], replicated, may hold values from -0.109375 to 0.109375
- b_final: float32 [64], replicated, may hold values from -3 to 3
- latent: float32 [8192, 64], P(('groups', 'patch', 'cfg', 'head')), parts along dimension 0, may hold values from -6 to 6
- prev_denoised: float32 [8192, 64], P(('groups', 'patch', 'cfg', 'head')), parts along dimension 0, may hold values from -24 to 24
- guidance: float32 [2], P('groups'), parts along dimension 0, may hold values from 2 to 5
- step_index: int32 [1], replicated, may hold values from 14 to 21
- step_count: int32 [1], replicated, may hold values from 24 to 27
Outputs:
- fresh_kv: bfloat16 [2, 2, 8704, 1536], P('cfg', None, ('groups', 'patch'), 'head'), parts along dimension 2
- next_latent: float32 [8192, 64], P(('groups', 'patch', 'cfg', 'head')), parts along dimension 0
- denoised: float32 [8192, 64], P(('groups', 'patch', 'cfg', 'head')), parts along dimension 0
There are 2 independent parts, one for each index of `groups`. A program takes and returns all parts, laid end to end along the dimension named above; an argument that names none is the same for every part. Nothing has to cross between parts.
All inputs are finite; a program needn't handle non-finite values.
Results may differ from a plain program's by a relative error of at most 0.0075.
The roundings to bfloat16 on the way count: a program that leaves them out, or rounds other values in their place, can miss the bound.
Values may be sent and summed in bfloat16 or wider, within the bound.
A program may use at most 128 MiB of HBM per device.

v0:
```python
import math

import jax
import jax.numpy as jnp
from jax import lax
from jax.sharding import PartitionSpec as P

D = 3072
HD = 128
CH = 64
GRID_W = 128


epsilon = 1e-06
time_shift = 3.0


def in_blocks(x, dim, peers):
    lengths = x.shape
    tiles = x.reshape(*lengths[:dim], peers, lengths[dim] // peers, *lengths[dim + 1 :])
    return jnp.moveaxis(tiles, dim, 0)


def sent_and_summed(x, axis, dim):
    peers = lax.axis_size(axis)
    tiles = lax.all_to_all(in_blocks(x, dim, peers), axis, 0, 0, tiled=True)
    return jnp.sum(tiles.astype(jnp.float32), axis=0)


def swapped(x, axis, bit):
    return lax.ppermute(x, axis, [(i, i ^ 1 << bit) for i in range(lax.axis_size(axis))])


def layer_norm(values):
    mean_val = jnp.mean(values, axis=-1, keepdims=True)
    centered = values - mean_val
    variance = jnp.mean(centered * centered, axis=-1, keepdims=True)
    return centered * lax.rsqrt(variance + epsilon)


def rms_norm(values, gain_vec):
    return (
        values * lax.rsqrt(jnp.mean(values * values, axis=-1, keepdims=True) + epsilon) * gain_vec
    )


def rotate(values, positions, grid_width):
    quarter = values.shape[-1] // 4
    freqs = 10000.0 ** (-jnp.arange(quarter, dtype=jnp.float32) / quarter)
    row_pos = (positions // grid_width).astype(jnp.float32)
    col_pos = (positions % grid_width).astype(jnp.float32)
    angles = jnp.stack(
        [row_pos[:, None] * freqs[None, :], col_pos[:, None] * freqs[None, :]], axis=1
    )
    cosine = jnp.cos(angles)[:, None]
    sine = jnp.sin(angles)[:, None]
    shaped = values.reshape(values.shape[0], values.shape[1], 2, 2, quarter)
    first = shaped[:, :, :, 0]
    second = shaped[:, :, :, 1]
    turned = jnp.stack([first * cosine - second * sine, second * cosine + first * sine], axis=3)
    return turned.reshape(values.shape)


def noise_level(index, count):
    frac = 1.0 - index / count
    lift = math.exp(time_shift)
    return lift * frac / (lift * frac + 1.0 - frac)


def log_ratio(sigma_val):
    return jnp.log(1.0 - sigma_val) - jnp.log(sigma_val)


def solver_step(cond, uncond, guidance, step_index, step_count, latent, prev_denoised):
    guided = uncond + guidance[0] * (cond - uncond)
    index = step_index[0].astype(jnp.float32)
    count = step_count[0].astype(jnp.float32)
    sigma_prev = noise_level(index - 1.0, count)
    sigma_now = noise_level(index, count)
    sigma_next = noise_level(index + 1.0, count)
    step_now = log_ratio(sigma_next) - log_ratio(sigma_now)
    step_prev = log_ratio(sigma_now) - log_ratio(sigma_prev)
    ratio = step_prev / step_now
    denoised = latent - sigma_now * guided
    blend = (1.0 + 0.5 / ratio) * denoised - 0.5 / ratio * prev_denoised
    next_latent = (
        sigma_next / sigma_now * latent - (1.0 - sigma_next) * (jnp.exp(-step_now) - 1.0) * blend
    )
    return (next_latent, denoised)


def body(
    img_hidden,
    txt_hidden,
    modulation,
    w_qkv,
    q_gain,
    k_gain,
    w_out,
    b_out,
    stale_kv,
    final_mod,
    w_final,
    b_final,
    latent,
    prev_denoised,
    guidance,
    step_index,
    step_count,
):
    head_width = w_out.shape[0]
    head_count = head_width // HD
    img_rows = img_hidden.shape[1]
    txt_rows = txt_hidden.shape[1]
    kv_rows = img_rows + txt_rows
    out_rows = latent.shape[0]
    patch_index = lax.axis_index("patch")
    cfg_index = lax.axis_index("cfg")
    head_index = lax.axis_index("head")
    head_total = lax.axis_size("head")
    inv_root = HD ** (-0.5)
    shift_vec = modulation[0, 0]
    scale_vec = modulation[0, 1]
    gate_vec = modulation[0, 2]
    modded_img = (
        layer_norm(img_hidden[0].astype(jnp.float32)) * (1.0 + scale_vec) + shift_vec
    ).astype(jnp.bfloat16)
    modded_txt = (
        layer_norm(txt_hidden[0].astype(jnp.float32)) * (1.0 + scale_vec) + shift_vec
    ).astype(jnp.bfloat16)
    weight_flat = w_qkv.reshape(D, 3 * head_width)
    proj_img = jnp.dot(modded_img, weight_flat, preferred_element_type=jnp.float32).reshape(
        img_rows, 3, head_count, HD
    )
    proj_txt = jnp.dot(modded_txt, weight_flat, preferred_element_type=jnp.float32).reshape(
        txt_rows, 3, head_count, HD
    )
    positions = patch_index * img_rows + jnp.arange(img_rows, dtype=jnp.int32)
    queries = rotate(rms_norm(proj_img[:, 0], q_gain), positions, GRID_W).astype(jnp.bfloat16)
    img_keys = rotate(rms_norm(proj_img[:, 1], k_gain), positions, GRID_W).astype(jnp.bfloat16)
    img_vals = proj_img[:, 2].astype(jnp.bfloat16)
    txt_keys = rms_norm(proj_txt[:, 1], k_gain).astype(jnp.bfloat16)
    txt_vals = proj_txt[:, 2].astype(jnp.bfloat16)
    fresh_keys = jnp.concatenate([txt_keys, img_keys], axis=0)
    fresh_vals = jnp.concatenate([txt_vals, img_vals], axis=0)
    fresh_kv = jnp.stack(
        [fresh_keys.reshape(kv_rows, head_width), fresh_vals.reshape(kv_rows, head_width)]
    )[None]

    def scores_of(key_block):
        return (
            jnp.einsum("qhd,khd->hqk", queries, key_block, preferred_element_type=jnp.float32)
            * inv_root
        )

    own_scores = scores_of(fresh_keys)
    own_top = jnp.max(own_scores, axis=-1)
    own_expo = jnp.exp(own_scores - own_top[..., None])
    own_total = jnp.sum(own_expo, axis=-1)
    own_acc = jnp.einsum(
        "hqk,khd->hqd",
        own_expo.astype(jnp.bfloat16),
        fresh_vals,
        preferred_element_type=jnp.float32,
    )
    own_first = patch_index * kv_rows
    block_piece = lax.all_gather(stale_kv, "patch", axis=2, tiled=True)
    key_count = block_piece.shape[2]
    key_block = block_piece[0, 0].reshape(key_count, head_count, HD)
    val_block = block_piece[0, 1].reshape(key_count, head_count, HD)
    scores = scores_of(key_block)
    row_ids = jnp.arange(key_count, dtype=jnp.int32)
    mine = (row_ids >= own_first) & (row_ids < own_first + kv_rows)
    scores = jnp.where(mine[None, None, :], -1e30, scores)
    top_new = jnp.maximum(own_top, jnp.max(scores, axis=-1))
    factor = jnp.exp(own_top - top_new)
    expo = jnp.exp(scores - top_new[..., None])
    total_new = own_total * factor + jnp.sum(expo, axis=-1)
    acc_new = own_acc * factor[..., None] + jnp.einsum(
        "hqk,khd->hqd", expo.astype(jnp.bfloat16), val_block, preferred_element_type=jnp.float32
    )
    attn = (
        (acc_new / total_new[..., None])
        .transpose(1, 0, 2)
        .reshape(img_rows, head_width)
        .astype(jnp.bfloat16)
    )
    hidden_in = img_hidden[0]
    ordered_attn = (
        attn.reshape(2, head_total, out_rows, head_width)
        .transpose(1, 0, 2, 3)
        .reshape(img_rows, head_width)
    )
    projected = sent_and_summed(
        jnp.dot(ordered_attn, w_out, preferred_element_type=jnp.float32).astype(jnp.bfloat16),
        "head",
        0,
    )
    own_hidden = lax.dynamic_index_in_dim(
        hidden_in.reshape(2, head_total, out_rows, D), head_index, 1, keepdims=False
    ).reshape(2 * out_rows, D)
    mixed = own_hidden.astype(jnp.float32) + gate_vec * (projected + b_out)
    final_in = (layer_norm(mixed) * (1.0 + final_mod[0, 1]) + final_mod[0, 0]).astype(jnp.bfloat16)
    velocity = (jnp.dot(final_in, w_final, preferred_element_type=jnp.float32) + b_final).reshape(
        2, out_rows, CH
    )
    partner = swapped(velocity, "cfg", 0)
    own_rows = lax.dynamic_index_in_dim(velocity, cfg_index, 0, keepdims=False)
    partner_rows = lax.dynamic_index_in_dim(partner, cfg_index, 0, keepdims=False)
    cond = jnp.where(cfg_index == 0, own_rows, partner_rows)
    uncond = jnp.where(cfg_index == 0, partner_rows, own_rows)
    next_latent, denoised = solver_step(
        cond, uncond, guidance, step_index, step_count, latent, prev_denoised
    )
    return (fresh_kv, next_latent, denoised)


def solution(mesh):
    return jax.shard_map(
        body,
        mesh=mesh,
        in_specs=(
            P("cfg", ("groups", "patch"), None),
            P("cfg", ("groups", "patch"), None),
            P(("groups", "cfg"), None, None),
            P(None, None, "head"),
            P(),
            P(),
            P("head", None),
            P(),
            P("cfg", None, ("groups", "patch"), "head"),
            P(("groups", "cfg"), None, None),
            P(),
            P(),
            P(("groups", "patch", "cfg", "head"), None),
            P(("groups", "patch", "cfg", "head"), None),
            P("groups"),
            P(),
            P(),
        ),
        out_specs=(
            P("cfg", None, ("groups", "patch"), "head"),
            P(("groups", "patch", "cfg", "head"), None),
            P(("groups", "patch", "cfg", "head"), None),
        ),
        check_vma=False,
    )
```

profile of v0, /device:TPU:33, one launch (start us, length us, event | category | flops | bytes accessed | tf_op | source)
XLA Modules:
  0.0 220.0 jit_solution(4321389743603134770)
XLA Ops:
  7.3 2.2 %copy.56 = bf16[1,2,272,384]{3,1,0,2:T(2,128)(2,1)} copy(bf16[1,2,272,384]{3,2,1,0:T(8,128)(2,1)} %param.25) | data formatting | bytes 835584 | tf_op args[8]
  9.6 10.1 %copy.46 = bf16[3072,3,384]{0,2,1:T(8,128)(2,1)} copy(bf16[3072,3,384]{2,0,1:T(8,128)(2,1)} %param.20) | data formatting | bytes 14155776 | tf_op args[3]
  20.2 5.0 %fusion.51 = f32[16,3,3,128]{3,0,2,1:T(8,128)S(1)} fusion(bf16[3,3,128,3072]{3,2,1,0:T(8,128)(2,1)} %bitcast.140, bf16[1,16,3072]{2,1,0:T(8,128)(2,1)S(1)} %copy-done.5, f32[3072]{0:T(1024)S(1)} %bitcast.169, f32[3072]{0:T(1024)S(1)} %bitcast.167, f32[16]{0:T(128)S(1)} %add_rsqrt_fusion.5, f32[16]{0:T(128)S(1)} %broadcast_multiply_fusion.4), kind=kOutput, calls=%fused_computation.76 | convolution fusion | flops 113541120 | bytes 7274624 | tf_op jit(solution)/shard_map/dot_general | solution.py:135
  28.2 1.7 convert_reduce_fusion
  29.9 2.0 fusion.12
  31.9 5.7 %fusion.14 = f32[256,3,3,128]{0,3,2,1:T(8,128)S(1)} fusion(bf16[3,3,128,3072]{3,2,1,0:T(8,128)(2,1)} %bitcast.141, bf16[1,256,3072]{2,1,0:T(8,128)(2,1)} %param.17, f32[3072]{0:T(1024)S(1)} %bitcast.170, f32[3072]{0:T(1024)S(1)} %bitcast.168, f32[256]{0:T(256)S(1)} %add_rsqrt_fusion.4, f32[256]{0:T(256)S(1)} %broadcast_multiply_fusion.3), kind=kOutput, calls=%fused_computation.20 | convolution fusion | flops 1816657920 | bytes 9857024 | tf_op jit(solution)/shard_map/dot_general | solution.py:132
  43.9 1.7 slice_bitcast_fusion.1
  45.6 65.8 %all-gather.2.cloned.1.call-done = bf16[1,2,4352,384]{3,1,0,2:T(2,128)(2,1)} async-done(((bf16[1,2,272,384]{3,1,0,2:T(2,128)(2,1)}), bf16[1,2,4352,384]{3,1,0,2:T(2,128)(2,1)}) %all-gather.2.cloned.1.call-update) | async-done | bytes 6684688 | tf_op jit(solution)/shard_map/all_gather | solution.py:167
  111.4 14.7 %fusion.77 = (bf16[1,1,4352,384]{3,1,0,2:T(2,128)(2,1)}, bf16[1,1,4352,384]{3,1,0,2:T(2,128)(2,1)}) fusion(bf16[1,2,4352,384]{3,1,0,2:T(2,128)(2,1)} %all-gather.2.cloned.1.call-done), kind=kLoop, calls=%fused_computation.133 | loop fusion | bytes 13369344 | tf_op jit(solution)/shard_map/slice | solution.py:169
  126.2 14.2 %copy.75 = bf16[1,1,4352,384]{2,3,1,0:T(8,128)(2,1)} copy(bf16[1,1,4352,384]{3,1,0,2:T(2,128)(2,1)} %get-tuple-element.15) | data formatting | bytes 6684672
  140.3 14.2 %copy.76 = bf16[1,1,4352,384]{2,3,1,0:T(8,128)(2,1)} copy(bf16[1,1,4352,384]{3,1,0,2:T(2,128)(2,1)} %get-tuple-element.16) | data formatting | bytes 6684672
  154.6 4.3 %fusion = (f32[3,256]{1,0:T(4,128)S(1)}, f32[3,256,4352]{2,1,0:T(8,128)S(1)}) fusion(pred[4352]{0:T(1024)(128)(4,1)S(1)} %fusion.62, bf16[256,3,128]{0,2,1:T(8,128)(2,1)S(1)} %bitcast.151, bf16[4352,3,128]{0,2,1:T(8,128)(2,1)} %bitcast.142), kind=kOutput, calls=%fused_computation.2 | convolution fusion | flops 865664256 | bytes 16915712 | tf_op jit(solution)/shard_map/qhd,khd->hqk/dot_general | solution.py:152
  158.8 3.0 %fusion.1 = f32[3,256]{1,0:T(4,128)S(1)} fusion(f32[3,256,4352]{2,1,0:T(8,128)S(1)} %get-tuple-element.34, f32[3,256]{1,0:T(4,128)S(1)} %max.18, pred[4352]{0:T(1024)(128)(4,1)S(1)} %fusion.62), kind=kLoop, calls=%fused_computation.3 | loop fusion | flops 13368576 | bytes 13379840 | tf_op jit(solution)/shard_map/reduce_sum | solution.py:178
  161.8 1.8 copy-done.1
  163.6 7.4 %fusion.20 = f32[256,3,128]{2,0,1:T(8,128)S(1)} fusion(bf16[4352,3,128]{0,2,1:T(8,128)(2,1)} %bitcast.149, f32[3,256,4352]{2,1,0:T(8,128)} %copy-done.1, f32[3,256]{1,0:T(4,128)S(1)} %max.18, pred[4352]{0:T(1024)(128)(4,1)S(1)} %fusion.62), kind=kOutput, calls=%fused_computation.26 | convolution fusion | flops 869007360 | bytes 17112320 | tf_op jit(solution)/shard_map/hqk,khd->hqd/dot_general | solution.py:179
  172.0 2.1 convolution_convert_fusion
  174.2 4.6 %all-to-all-start = ((bf16[4,64,3072]{2,1,0:T(8,128)(2,1)}), bf16[4,64,3072]{2,1,0:T(8,128)(2,1)}, u32[]{:S(2)}, u32[]{:S(2)}) async-start(bf16[4,64,3072]{2,1,0:T(8,128)(2,1)} %bitcast.148), calls=%async_computation | async-start | bytes 3145728 | tf_op jit(solution)/shard_map/all_to_all | solution.py:26
  179.7 1.9 dynamic-slice_convert_fusion
  181.6 16.5 %all-to-all-done = bf16[4,64,3072]{2,1,0:T(8,128)(2,1)} async-done(((bf16[4,64,3072]{2,1,0:T(8,128)(2,1)}), bf16[4,64,3072]{2,1,0:T(8,128)(2,1)}, u32[]{:S(2)}, u32[]{:S(2)}) %all-to-all-start) | async-done | bytes 1572896 | tf_op jit(solution)/shard_map/all_to_all | solution.py:26
  198.2 1.7 convert_reduce_fusion.1
  201.2 1.3 multiply_reduce_fusion
  202.6 1.4 fusion.31
  205.3 2.3 %collective-permute-start = (f32[2,32,64]{2,1,0:T(8,128)S(1)}, f32[2,32,64]{2,1,0:T(8,128)S(1)}, u32[]{:S(2)}, u32[]{:S(2)}) collective-permute-start(f32[2,32,64]{2,1,0:T(8,128)S(1)} %bitcast.163), channel_id=1, source_target_pairs={{0,4},{4,0},{1,5},{5,1},{2,6},{6,2},{3,7},{7,3},{8,12},{12,8},{9,1... | collective-permute-start | bytes 49160 | tf_op jit(solution)/shard_map/ppermute | solution.py:31
  207.6 1.3 maximum_bitcast_fusion
  (100 shorter events, 16.0 us)
Async XLA Ops:
  7.2 164.8 %copy-start = (bf16[384,3072]{1,0:T(8,128)(2,1)S(1)}, bf16[384,3072]{1,0:T(8,128)(2,1)}, u32[]{:S(2)}) copy-start(bf16[384,3072]{1,0:T(8,128)(2,1)} %param.23) | copy-start | bytes 7077892
  7.2 104.2 %all-gather.2.cloned.1.call-start = ((), (), s32[]{:S(2)}) async-start(), calls=%async_computation.1 | async-start | bytes 7102464 | tf_op jit(solution)/shard_map/all_gather | solution.py:167
  9.6 10.2 %copy-start.5 = (bf16[1,16,3072]{2,1,0:T(8,128)(2,1)S(1)}, bf16[1,16,3072]{2,1,0:T(8,128)(2,1)}, u32[]{:S(2)}) copy-start(bf16[1,16,3072]{2,1,0:T(8,128)(2,1)} %param.18) | copy-start | bytes 294916
  9.6 10.5 %copy-start.12 = (f32[1,3,3072]{2,0,1:T(1,128)S(1)}, f32[1,3,3072]{2,0,1:T(1,128)}, u32[]{:S(2)}) copy-start(f32[1,3,3072]{2,0,1:T(1,128)} %param.19) | copy-start | bytes 110596
  20.1 5.0 %copy-start.18 = (f32[128]{0:T(128)S(1)}, f32[128]{0:T(128)}, u32[]{:S(2)}) copy-start(f32[128]{0:T(128)} %param.21) | copy-start | bytes 1540
  20.1 5.7 %copy-start.16 = (f32[128]{0:T(128)S(1)}, f32[128]{0:T(128)}, u32[]{:S(2)}) copy-start(f32[128]{0:T(128)} %param.22) | copy-start | bytes 1540
  25.1 12.5 %copy-start.6 = (f32[16,3,3,128]{3,0,2,1:T(8,128)}, f32[16,3,3,128]{3,0,2,1:T(8,128)S(1)}, u32[]{:S(2)}) copy-start(f32[16,3,3,128]{3,0,2,1:T(8,128)S(1)} %fusion.51) | copy-start | bytes 221188
  37.6 1.4 copy-start.4
  38.8 5.0 %copy-start.17 = (f32[128]{0:T(128)S(1)}, f32[128]{0:T(128)}, u32[]{:S(2)}) copy-start(f32[128]{0:T(128)} %param.22) | copy-start | bytes 1540
  42.8 0.9 copy-start.2
  158.8 4.7 %copy-start.1 = (f32[3,256,4352]{2,1,0:T(8,128)}, f32[3,256,4352]{2,1,0:T(8,128)S(1)}, u32[]{:S(2)}) copy-start(f32[3,256,4352]{2,1,0:T(8,128)S(1)} %get-tuple-element.34) | copy-start | bytes 40108036
  163.5 7.4 %copy-start.3 = (f32[3,256,272]{1,2,0:T(8,128)S(1)}, f32[3,256,272]{1,2,0:T(8,128)}, u32[]{:S(2)}) copy-start(f32[3,256,272]{1,2,0:T(8,128)} %copy-done.2) | copy-start | bytes 2506756
  163.6 7.4 %copy-start.7 = (bf16[256,3,128]{0,2,1:T(8,128)(2,1)S(1)}, bf16[256,3,128]{0,2,1:T(8,128)(2,1)}, u32[]{:S(2)}) copy-start(bf16[256,3,128]{0,2,1:T(8,128)(2,1)} %slice_bitcast_fusion.1) | copy-start | bytes 589828
  163.6 7.4 %copy-start.9 = (bf16[16,3,128]{0,2,1:T(8,128)(2,1)S(1)}, bf16[16,3,128]{0,2,1:T(8,128)(2,1)}, u32[]{:S(2)}) copy-start(bf16[16,3,128]{0,2,1:T(8,128)(2,1)} %copy.54) | copy-start | bytes 36868
  172.0 6.7 %copy-start.10 = (f32[1,16,384]{2,1,0:T(8,128)S(1)}, f32[1,16,384]{2,1,0:T(8,128)}, u32[]{:S(2)}) copy-start(f32[1,16,384]{2,1,0:T(8,128)} %squeeze.14) | copy-start | bytes 73732
  172.0 6.7 %copy-start.11 = (f32[1,16,384]{2,1,0:T(8,128)S(1)}, f32[1,16,384]{2,1,0:T(8,128)}, u32[]{:S(2)}) copy-start(f32[1,16,384]{2,1,0:T(8,128)} %mul.390) | copy-start | bytes 73732
  172.0 9.6 %copy-start.13 = (f32[1,2,3072]{2,1,0:T(2,128)S(1)}, f32[1,2,3072]{2,1,0:T(2,128)}, u32[]{:S(2)}) copy-start(f32[1,2,3072]{2,1,0:T(2,128)} %param.26) | copy-start | bytes 73732
  174.2 25.7 %copy-start.8 = (f32[3072]{0:T(1024)S(1)}, f32[3072]{0:T(1024)}, u32[]{:S(2)}) copy-start(f32[3072]{0:T(1024)} %param.24) | copy-start | bytes 36868
  174.2 24.0 %all-to-all-start = ((bf16[4,64,3072]{2,1,0:T(8,128)(2,1)}), bf16[4,64,3072]{2,1,0:T(8,128)(2,1)}, u32[]{:S(2)}, u32[]{:S(2)}) async-start(bf16[4,64,3072]{2,1,0:T(8,128)(2,1)} %bitcast.148), calls=%async_computation | async-start | bytes 3145728 | tf_op jit(solution)/shard_map/all_to_all | solution.py:26
  181.6 22.4 %copy-start.19 = (f32[64]{0:T(128)S(1)}, f32[64]{0:T(128)}, u32[]{:S(2)}) copy-start(f32[64]{0:T(128)} %param.28) | copy-start | bytes 772
  201.2 11.3 %copy-start.14 = (f32[32,64]{1,0:T(8,128)S(1)}, f32[32,64]{1,0:T(8,128)}, u32[]{:S(2)}) copy-start(f32[32,64]{1,0:T(8,128)} %param.30) | copy-start | bytes 24580
  201.2 11.3 %copy-start.15 = (f32[32,64]{1,0:T(8,128)S(1)}, f32[32,64]{1,0:T(8,128)}, u32[]{:S(2)}) copy-start(f32[32,64]{1,0:T(8,128)} %param.29) | copy-start | bytes 24580
  205.3 7.2 %collective-permute-start = (f32[2,32,64]{2,1,0:T(8,128)S(1)}, f32[2,32,64]{2,1,0:T(8,128)S(1)}, u32[]{:S(2)}, u32[]{:S(2)}) collective-permute-start(f32[2,32,64]{2,1,0:T(8,128)S(1)} %bitcast.163), channel_id=1, source_target_pairs={{0,4},{4,0},{1,5},{5,1},{2,6},{6,2},{3,7},{7,3},{8,12},{12,8},{9,1... | collective-permute-start | bytes 49160 | tf_op jit(solution)/shard_map/ppermute | solution.py:31
Sparse Core Ops, SparseCore 0:
  10.4 100.9 all-gather.1
where the time goes:
time: 222 us; the launch traced here: 220 us
  waiting for transfers between devices  82.4 us (37%)
  local copies, waits for them, and re-layouts  66.9 us (30%)
  matrix products  27.5 us (12%)
  other arithmetic  19.1 us (9%)
  between operations  17.1 us (8%)
  starting transfers between devices  6.96 us (3%)
    all_gather x1, waiting for transfers between devices, body(): block_piece = lax.all_gather(stale_kv, 'patch', axis=2, tiled=True)  65.8 us
    unnamed x46, local copies, waits for them, and re-layouts  44.6 us
    all_to_all x1, waiting for transfers between devices, sent_and_summed(): tiles = lax.all_to_all(in_blocks(x, dim, peers), axis, 0, 0, tiled=True)  16.5 us
    slice x1, local copies, waits for them, and re-layouts, body(): key_block = block_piece[0, 0].reshape(key_count, head_count, HD)  14.7 us
    dot_general x1, matrix products, body(): jnp.einsum('hqk,khd->hqd', expo.astype(jnp.bfloat16), val_block, preferre...  7.36 us
    dot_general x1, matrix products, body(): jnp.dot(modded_img, weight_flat, preferred_element_type=jnp.float32)  5.72 us
    dot_general x2, matrix products, scores_of(): jnp.einsum('qhd,khd->hqk', queries, key_block, preferred_element_type=jnp...  5.46 us
    dot_general x1, matrix products, body(): jnp.dot(modded_txt, weight_flat, preferred_element_type=jnp.float32)  4.95 us
  transfers between devices with their start and end apart: 3, of which 2 were waited for; matrix products, arithmetic and copies ran while one was open for 18% of the time, Pallas kernels for 0%

commit v1 on v0

v1 whole, which is shorter than its diff:
```python
import functools
import math

import jax
import jax.numpy as jnp
import numpy as np
from jax import lax
from jax.experimental import pallas as pl
from jax.experimental.pallas import tpu as pltpu
from jax.sharding import PartitionSpec as P

HD = 128
GRID_W = 128
EPS = 1e-06
TIME_SHIFT = 3.0
MESH = pl.DeviceIdType.MESH
BF = jnp.bfloat16
F32 = jnp.float32


def rotation_tables(grid_rows):
    quarter = HD // 4
    freqs = 10000.0 ** (-np.arange(quarter, dtype=np.float32) / quarter)
    freqs = freqs.astype(np.float32)

    def half(count, at):
        angle = np.arange(count, dtype=np.float32)[:, None] * freqs[None, :]
        out = np.zeros((3, count, HD), np.float32)
        cosine = np.cos(angle.astype(np.float64))
        sine = np.sin(angle.astype(np.float64))
        out[0, :, at : at + quarter] = cosine
        out[0, :, at + quarter : at + 2 * quarter] = cosine
        out[1, :, at : at + quarter] = -sine
        out[2, :, at + quarter : at + 2 * quarter] = sine
        return out

    return half(grid_rows, 0), half(GRID_W, 2 * quarter)


def normed(values):
    mean = jnp.mean(values, axis=-1, keepdims=True)
    centered = values - mean
    variance = jnp.mean(centered * centered, axis=-1, keepdims=True)
    return centered * lax.rsqrt(variance + EPS)


def noise_level(index, count):
    frac = 1.0 - index / count
    lift = math.exp(TIME_SHIFT)
    return lift * frac / (lift * frac + 1.0 - frac)


def log_ratio(sigma):
    return jnp.log(1.0 - sigma) - jnp.log(sigma)


def kernel(
    sizes,
    img_hbm, txt_hbm, mod_hbm, wqkv_hbm, qg_hbm, kg_hbm, wout_hbm, bout_hbm, stale_hbm,
    fmod_hbm, wfin_hbm, bfin_hbm, lat_hbm, prev_hbm, rowtab_hbm, coltab_hbm,
    guidance, step_index, step_count,
    fresh_hbm, next_ref, den_ref,
    img, txt, mod, wqkv, qg, kg, bout, fmod, wfin, bfin, lat, prev, rowtab, coltab,
    modded, proj, tabs, fresh, qT, top, total, acc,
    fl, fr, wbuf, asend, arecv, mixed, final_in, vel, vel_in,
    in_sem, fresh_sem, ring_send, ring_recv, w_send, w_recv, d_send, d_recv, a_send, a_recv,
    v_send, v_recv,
):
    n_patch, n_head = sizes
    last = n_patch // 2
    p = lax.axis_index("patch")
    c = lax.axis_index("cfg")
    x = lax.axis_index("head")
    right, left = lax.rem(p + 1, n_patch), lax.rem(p + n_patch - 1, n_patch)
    other = 1 - c
    ups = [lax.rem(x + k, n_head) for k in range(n_head)]
    width = wout_hbm.shape[0]
    heads = width // HD
    depth = img.shape[1]
    rows = img.shape[0]
    trows = txt.shape[0]
    half_w = depth // 2
    out_rows = lat.shape[0]
    inv_root = HD ** (-0.5)

    pairs = [
        (img_hbm, img), (txt_hbm, txt), (mod_hbm, mod),
        (wqkv_hbm.at[0], wqkv.at[0]), (wqkv_hbm.at[1], wqkv.at[1]), (wqkv_hbm.at[2], wqkv.at[2]),
        (rowtab_hbm, rowtab), (coltab_hbm, coltab), (qg_hbm, qg), (kg_hbm, kg),
        (bout_hbm, bout), (fmod_hbm, fmod), (wfin_hbm, wfin), (bfin_hbm, bfin),
        (lat_hbm, lat), (prev_hbm, prev),
        (wout_hbm.at[:, pl.ds(0, half_w)], wbuf.at[0, pl.ds(0, width)]),
        (wout_hbm.at[:, pl.ds(half_w, half_w)], wbuf.at[1, pl.ds(0, width)]),
    ]
    reads = [pltpu.make_async_copy(s, d, in_sem.at[i]) for i, (s, d) in enumerate(pairs)]
    for r in reads:
        r.start()

    barrier = pltpu.get_barrier_semaphore()
    peers = [{"patch": right}, {"patch": left}, {"cfg": other}] + [{"head": u} for u in ups[1:]]
    for peer in peers:
        pl.semaphore_signal(barrier, inc=1, device_id=peer, device_id_type=MESH)
    pl.semaphore_wait(barrier, len(peers))

    def hop(side, stage, h, kv):
        if isinstance(stage, int) and stage == 1:
            src = stale_hbm.at[kv, :, pl.ds(pl.multiple_of(h * HD, HD), HD)]
        else:
            src = (fl, fr)[side].at[stage - 2, h, kv]
        if isinstance(stage, int) and stage == last:
            dst = fl.at[stage - 1, h, kv]
        else:
            dst = (fl, fr)[side].at[stage - 1, h, kv]
        return pltpu.make_async_remote_copy(
            src_ref=src, dst_ref=dst,
            send_sem=ring_send.at[side, stage - 1, h, kv],
            recv_sem=ring_recv.at[side, stage - 1, h, kv],
            device_id={"patch": (right, left)[side]}, device_id_type=MESH,
        )

    pieces = [(h, kv) for h in range(heads) for kv in range(2)]
    cut = len(pieces) // 2
    final_pieces = (pieces[:cut], pieces[cut:])

    for h, kv in pieces:
        for side in range(2):
            hop(side, 1, h, kv).start()

    def forward(stage, h):
        for kv in range(2):
            for side in range(2):
                hop(side, stage, h, kv).wait_recv()
                hop(side, stage + 1, h, kv).start()

    def w_copy(i, src, dst, send, recv, dev):
        return pltpu.make_async_remote_copy(
            src_ref=src, dst_ref=dst, send_sem=send.at[i], recv_sem=recv.at[i],
            device_id=dev, device_id_type=MESH,
        )

    my_cols = wout_hbm.at[:, pl.ds(pl.multiple_of(c * half_w, 128), half_w)]
    hw = width // 2
    w1 = w_copy(0, my_cols, wbuf.at[c, pl.ds(width, width)], w_send, w_recv, {"head": ups[1]})
    w3 = w_copy(1, my_cols, wbuf.at[c, pl.ds(3 * width, width)], w_send, w_recv, {"head": ups[3]})
    w2a = w_copy(2, wbuf.at[c, pl.ds(width, hw)], wbuf.at[c, pl.ds(2 * width, hw)],
                 w_send, w_recv, {"head": ups[1]})
    w2b = w_copy(3, wbuf.at[c, pl.ds(3 * width + hw, hw)], wbuf.at[c, pl.ds(2 * width + hw, hw)],
                 w_send, w_recv, {"head": ups[3]})
    d_out = [w_copy(k - 1, wbuf.at[c, pl.ds(k * width, width)], wbuf.at[c, pl.ds(k * width, width)],
                    d_send, d_recv, {"cfg": other}) for k in range(1, n_head)]
    d_in = [w_copy(k - 1, wbuf.at[other, pl.ds(k * width, width)],
                   wbuf.at[other, pl.ds(k * width, width)],
                   d_send, d_recv, {"cfg": other}) for k in range(1, n_head)]
    w1.start()
    w3.start()

    for r in reads[:3]:
        r.wait()
    block = 16

    def modulate(values):
        return (normed(values.astype(F32)) * (1.0 + mod[1]) + mod[0]).astype(BF)

    for i in range(trows // block):
        modded[pl.ds(i * block, block), :] = modulate(txt[pl.ds(i * block, block), :])

    def modulate_rows(i, carry):
        at = pl.multiple_of(i * block, block)
        modded[pl.ds(trows + at, block), :] = modulate(img[pl.ds(at, block), :])
        return carry

    lax.fori_loop(0, rows // block, modulate_rows, 0)

    def project(j, carry):
        pltpu.make_async_copy(wqkv_hbm.at[j], wqkv.at[j], in_sem.at[3 + j]).wait()
        proj[j] = jnp.dot(modded[...], wqkv[j], preferred_element_type=F32)
        return carry

    for j in range(3):
        project(j, 0)
        if j < heads:
            forward(1, j)
    for h in range(3, heads):
        forward(1, h)

    for r in reads[6:10]:
        r.wait()

    tabs[0, pl.ds(0, trows), :] = jnp.ones((trows, HD), F32)
    tabs[1, pl.ds(0, trows), :] = jnp.zeros((trows, HD), F32)
    tabs[2, pl.ds(0, trows), :] = jnp.zeros((trows, HD), F32)
    grid_rows = rows // GRID_W
    for t in range(3):
        for i in range(grid_rows):
            tabs[t, pl.ds(trows + i * GRID_W, GRID_W), :] = (
                coltab[t] + rowtab[t, pl.ds(p * grid_rows + i, 1), :]
            )

    quarter = HD // 4

    def turned(values, gain, first):
        scaled = values * lax.rsqrt(jnp.mean(values * values, axis=-1, keepdims=True) + EPS) * gain
        n = values.shape[0]
        return (
            scaled * tabs[0, pl.ds(first, n), :]
            + pltpu.roll(scaled, HD - quarter, 1) * tabs[1, pl.ds(first, n), :]
            + pltpu.roll(scaled, quarter, 1) * tabs[2, pl.ds(first, n), :]
        )

    for h in range(heads):
        cols = pl.ds(h * HD, HD)
        q = turned(proj[0, pl.ds(trows, rows), cols], qg[...], trows).astype(BF)
        qT[h] = q.T
        fresh[0, :, cols] = turned(proj[1, :, cols], kg[...], 0).astype(BF)
    fresh[1] = proj[2].astype(BF)
    fresh_out = pltpu.make_async_copy(fresh, fresh_hbm, fresh_sem.at[0])
    fresh_out.start()

    top[...] = jnp.full(top.shape, -1e30, F32)
    total[...] = jnp.zeros(total.shape, F32)
    acc[...] = jnp.zeros(acc.shape, F32)

    def attend(h, keys, vals):
        scores = jnp.dot(keys, qT[h], preferred_element_type=F32)
        old = top[h]
        new = jnp.maximum(old, jnp.max(scores, axis=0, keepdims=True))
        expo = jnp.exp((scores - new) * inv_root)
        factor = jnp.exp((old - new) * inv_root)
        top[h] = new
        total[h] = total[h] * factor + jnp.sum(expo, axis=0, keepdims=True)
        acc[h] = acc[h] * factor + lax.dot_general(
            vals, expo.astype(BF), (((0,), (0,)), ((), ())), preferred_element_type=F32
        )

    for h in range(heads):
        cols = pl.ds(h * HD, HD)
        attend(h, fresh[0, :, cols], fresh[1, :, cols])

    def both(stage, h):
        attend(h, fl[stage - 1, h, 0], fl[stage - 1, h, 1])
        attend(h, fr[stage - 1, h, 0], fr[stage - 1, h, 1])

    def step(stage, carry):
        def one(h, inner):
            forward(stage + 1, h)
            both(stage, h)
            return inner

        return lax.fori_loop(0, heads, one, carry)

    relay = (last - 2) // 2 + 1
    lax.fori_loop(1, relay, step, 0)
    w1.wait_recv()
    w2a.start()
    d_out[0].start()
    w3.wait_recv()
    w2b.start()
    d_out[2].start()
    lax.fori_loop(relay, last - 2, step, 0)

    for h in range(heads):
        for kv in range(2):
            for side in range(2):
                hop(side, last - 1, h, kv).wait_recv()
                if (h, kv) in final_pieces[side]:
                    hop(side, last, h, kv).start()
        both(last - 2, h)

    w2a.wait_recv()
    w2b.wait_recv()
    d_out[1].start()
    for r in reads[10:]:
        r.wait()

    def nearer(h, carry):
        both(last - 1, h)
        return carry

    lax.fori_loop(0, heads, nearer, 0)
    for copy in d_in:
        copy.wait_recv()

    for h in range(heads):
        for kv in range(2):
            for side in range(2):
                if (h, kv) in final_pieces[side]:
                    hop(side, last, h, kv).wait_recv()
        attend(h, fl[last - 1, h, 0], fl[last - 1, h, 1])
        out = (acc[h] / total[h]).astype(BF).T
        for part in range(2):
            for k in range(n_head):
                at = part * n_head * out_rows + k * out_rows
                asend[k, pl.ds(part * out_rows, out_rows), pl.ds(h * HD, HD)] = (
                    out[at : at + out_rows, :]
                )

    a_copies = [
        pltpu.make_async_remote_copy(
            src_ref=asend.at[ups[k]], dst_ref=arecv.at[:, pl.ds(k * width, width)],
            send_sem=a_send.at[k - 1], recv_sem=a_recv.at[k - 1],
            device_id={"head": ups[k]}, device_id_type=MESH,
        )
        for k in range(1, n_head)
    ]
    for k in (2, 1, 3):
        a_copies[k - 1].start()
    arecv[:, pl.ds(0, width)] = asend[x]
    for copy in a_copies:
        copy.wait_recv()

    chunk = 512
    attn = arecv[...]
    for n in range(depth // chunk):
        half, at = divmod(n * chunk, half_w)
        cols = pl.ds(n * chunk, chunk)
        projected = jnp.dot(attn, wbuf[half, :, pl.ds(at, chunk)], preferred_element_type=F32)
        for part in range(2):
            own = pl.ds(pl.multiple_of(part * n_head * out_rows + x * out_rows, out_rows), out_rows)
            mixed[pl.ds(part * out_rows, out_rows), cols] = img[own, cols].astype(F32) + mod[
                2, :, cols
            ] * (projected[part * out_rows : (part + 1) * out_rows] + bout[:, cols])

    def finish(i, carry):
        at = pl.multiple_of(i * block, block)
        final_in[pl.ds(at, block), :] = (
            normed(mixed[pl.ds(at, block), :]) * (1.0 + fmod[1:2, :]) + fmod[0:1, :]
        ).astype(BF)
        return carry

    lax.fori_loop(0, 2 * out_rows // block, finish, 0)
    velocity = (
        lax.dot_general(
            final_in[...], wfin[...], (((1,), (1,)), ((), ())), preferred_element_type=F32
        )
        + bfin[...]
    )
    ch = velocity.shape[1]
    vel[...] = jnp.zeros(vel.shape, F32)
    vel[0, :, pl.ds(0, ch)] = velocity[:out_rows]
    vel[1, :, pl.ds(0, ch)] = velocity[out_rows:]
    swap = pltpu.make_async_remote_copy(
        src_ref=vel.at[other], dst_ref=vel_in, send_sem=v_send.at[0], recv_sem=v_recv.at[0],
        device_id={"cfg": other}, device_id_type=MESH,
    )
    swap.start()

    index = jnp.full((1, ch), step_index[0], jnp.int32).astype(F32)
    count = jnp.full((1, ch), step_count[0], jnp.int32).astype(F32)
    scale = jnp.full((1, ch), guidance[0], F32)
    sigma_prev = noise_level(index - 1.0, count)
    sigma_now = noise_level(index, count)
    sigma_next = noise_level(index + 1.0, count)
    step_now = log_ratio(sigma_next) - log_ratio(sigma_now)
    step_prev = log_ratio(sigma_now) - log_ratio(sigma_prev)
    ratio = step_prev / step_now
    swap.wait_recv()
    mine = vel[c, :, pl.ds(0, ch)]
    theirs = vel_in[:, pl.ds(0, ch)]
    cond = jnp.where(c == 0, mine, theirs)
    uncond = jnp.where(c == 0, theirs, mine)
    guided = uncond + scale * (cond - uncond)
    denoised = lat[...] - sigma_now * guided
    blend = (1.0 + 0.5 / ratio) * denoised - 0.5 / ratio * prev[...]
    next_ref[...] = (
        sigma_next / sigma_now * lat[...] - (1.0 - sigma_next) * (jnp.exp(-step_now) - 1.0) * blend
    )
    den_ref[...] = denoised

    fresh_out.wait()
    for h, kv in pieces:
        for side in range(2):
            hop(side, 1, h, kv).wait_send()

    def drain(stage, carry):
        for h, kv in pieces:
            for side in range(2):
                hop(side, stage, h, kv).wait_send()
        return carry

    lax.fori_loop(2, last, drain, 0)
    for side in range(2):
        for h, kv in final_pieces[side]:
            hop(side, last, h, kv).wait_send()
    for copy in (w1, w3, w2a, w2b, *d_out, *a_copies, swap):
        copy.wait_send()


def body(
    sizes,
    img_hidden, txt_hidden, modulation, w_qkv, q_gain, k_gain, w_out, b_out, stale_kv,
    final_mod, w_final, b_final, latent, prev_denoised, guidance, step_index, step_count,
):
    n_patch, n_head = sizes
    rows, depth = img_hidden.shape[1:]
    trows = txt_hidden.shape[1]
    kv_rows = rows + trows
    width = w_out.shape[0]
    heads = width // HD
    out_rows, ch = latent.shape
    last = n_patch // 2
    n_rows = n_patch * rows // GRID_W
    rowtab, coltab = rotation_tables(n_rows)
    any_spec = pl.BlockSpec(memory_space=pl.ANY)
    smem = pl.BlockSpec(memory_space=pltpu.SMEM)
    vmem = pl.BlockSpec(memory_space=pltpu.VMEM)
    dma = pltpu.SemaphoreType.DMA
    V = pltpu.VMEM
    outs = pl.pallas_call(
        functools.partial(kernel, sizes),
        out_shape=(
            jax.ShapeDtypeStruct((2, kv_rows, width), BF),
            jax.ShapeDtypeStruct((out_rows, ch), F32),
            jax.ShapeDtypeStruct((out_rows, ch), F32),
        ),
        in_specs=[any_spec] * 16 + [smem] * 3,
        out_specs=(any_spec, vmem, vmem),
        scratch_shapes=[
            V((rows, depth), BF), V((trows, depth), BF), V((3, 1, depth), F32),
            V((3, depth, width), BF), V((1, HD), F32), V((1, HD), F32), V((1, depth), F32),
            V((2, depth), F32), V((ch, depth), BF), V((1, ch), F32), V((out_rows, ch), F32),
            V((out_rows, ch), F32), V((3, n_rows, HD), F32), V((3, GRID_W, HD), F32),
            V((kv_rows, depth), BF), V((3, kv_rows, width), F32), V((3, kv_rows, HD), F32),
            V((2, kv_rows, width), BF), V((heads, HD, rows), BF), V((heads, 1, rows), F32),
            V((heads, 1, rows), F32), V((heads, HD, rows), F32),
            V((last, heads, 2, kv_rows, HD), BF), V((last - 1, heads, 2, kv_rows, HD), BF),
            V((2, n_head * width, depth // 2), BF),
            V((n_head, 2 * out_rows, width), BF), V((2 * out_rows, n_head * width), BF),
            V((2 * out_rows, depth), F32), V((2 * out_rows, depth), BF),
            V((2, out_rows, 128), F32), V((out_rows, 128), F32),
            dma((18,)), dma((1,)),
            dma((2, last, heads, 2)), dma((2, last, heads, 2)),
            dma((4,)), dma((4,)), dma((n_head - 1,)), dma((n_head - 1,)),
            dma((n_head - 1,)), dma((n_head - 1,)), dma((1,)), dma((1,)),
        ],
        compiler_params=pltpu.CompilerParams(
            collective_id=0, has_side_effects=True, vmem_limit_bytes=60 * 1024 * 1024
        ),
    )(
        img_hidden[0], txt_hidden[0], modulation.transpose(1, 0, 2), w_qkv.transpose(1, 0, 2),
        q_gain[None], k_gain[None], w_out, b_out[None], stale_kv[0], final_mod[0], w_final.T,
        b_final[None], latent, prev_denoised, jnp.asarray(rowtab), jnp.asarray(coltab),
        guidance, step_index, step_count,
    )
    return outs[0][None], outs[1], outs[2]


def solution(mesh):
    sizes = (mesh.shape["patch"], mesh.shape["head"])
    rows4 = P(("groups", "patch", "cfg", "head"), None)
    return jax.shard_map(
        functools.partial(body, sizes),
        mesh=mesh,
        in_specs=(
            P("cfg", ("groups", "patch"), None),
            P("cfg", ("groups", "patch"), None),
            P(("groups", "cfg"), None, None),
            P(None, None, "head"),
            P(),
            P(),
            P("head", None),
            P(),
            P("cfg", None, ("groups", "patch"), "head"),
            P(("groups", "cfg"), None, None),
            P(),
            P(),
            rows4,
            rows4,
            P("groups"),
            P(),
            P(),
        ),
        out_specs=(P("cfg", None, ("groups", "patch"), "head"), rows4, rows4),
        check_vma=False,
    )
```

time: 222 us -> 115 us (0.52)
  Pallas kernels: 0 us -> 107 us
  waiting for transfers between devices: 82.4 us -> 0 us
  local copies, waits for them, and re-layouts: 66.9 us -> 4.45 us
  matrix products: 27.5 us -> 0 us
  other arithmetic: 19.1 us -> 0 us
  between operations: 17.1 us -> 2.58 us
  starting transfers between devices: 6.96 us -> 0 us
    pallas_call x0 -> x1, Pallas kernels: none -> 107 us  [body(): pl.pallas_call(functools.partial(kernel, sizes), out_shape=(jax.ShapeDtyp...]
    all_gather x1 -> x0, waiting for transfers between devices: 65.8 us -> none  [body(): block_piece = lax.all_gather(stale_kv, 'patch', axis=2, tiled=True)]
    unnamed x46 -> x3, local copies, waits for them, and re-layouts: 44.6 us -> 4.45 us
    dot_general x8 -> x0, matrix products: 27.5 us -> none  [the longest x1 7.36 us: body(): jnp.einsum('hqk,khd->hqd', expo.astype(jnp.bfloat16), val_block, preferre...]
    all_to_all x1 -> x0, waiting for transfers between devices: 16.5 us -> none  [sent_and_summed(): tiles = lax.all_to_all(in_blocks(x, dim, peers), axis, 0, 0, tiled=True)]
    slice x6 -> x0, local copies, waits for them, and re-layouts: 15.5 us -> none  [the longest x1 14.7 us: body(): key_block = block_piece[0, 0].reshape(key_count, head_count, HD)]
    reduce_sum x11 -> x0, other arithmetic: 11.5 us -> none  [the longest x3 3.47 us: layer_norm(): variance = jnp.mean(centered * centered, axis=-1, keepdims=True)]
    all_to_all x1 -> x0, starting transfers between devices: 4.56 us -> none  [sent_and_summed(): tiles = lax.all_to_all(in_blocks(x, dim, peers), axis, 0, 0, tiled=True)]
  transfers between devices with their start and end apart: 3 -> 0, of which waited for: 2 -> 0; matrix products, arithmetic and copies ran while one was open for 18% -> 0% of each run, Pallas kernels for 0% -> 0%
where the time goes in v1:
time: 115 us
  Pallas kernels  107 us (93%)
  local copies, waits for them, and re-layouts  4.45 us (4%)
  between operations  2.58 us (2%)
    pallas_call x1, Pallas kernels, body(): pl.pallas_call(functools.partial(kernel, sizes), out_shape=(jax.ShapeDtyp...  107 us
    unnamed x3, local copies, waits for them, and re-layouts  4.45 us

profile of v1, /device:TPU:33, one launch (start us, length us, event | category | flops | bytes accessed | tf_op | source)
XLA Modules:
  0.0 114.5 jit_solution(16996455147083968960)
XLA Ops:
  2.6 107.5 %shard_map.202 = (bf16[2,272,384]{2,1,0:T(8,128)(2,1)}, f32[32,64]{1,0:T(8,128)}, f32[32,64]{1,0:T(8,128)}) custom-call(bf16[256,3072]{1,0:T(8,128)(2,1)} %bitcast.13, bf16[16,3072]{1,0:T(8,128)(2,1)} %bitcast.17, f32[3,1,3072]{2,1,0:T(1,128)} %bitcast.18, bf16[3,3072,384]{2,1,0:T(8,128)(2,1)} %bitcast.12, f32[1,128]{1,0:T(1,128)} %bitcast.21, ...), custom_call_target="tpu_custom_call" | custom-call | tf_op jit(solution)/shard_map/pallas_call | solution.py:408
  110.1 1.8 %copy.28 = bf16[1,2,272,384]{3,2,1,0:T(8,128)(2,1)} copy(bf16[1,2,272,384]{3,2,1,0:T(8,128)(2,1)} %bitcast.14) | data formatting | bytes 835584
  111.9 1.3 %copy.29 = f32[32,64]{1,0:T(8,128)} copy(f32[32,64]{1,0:T(8,128)} %get-tuple-element.13) | data formatting | bytes 16384
  113.2 1.3 %copy.30 = f32[32,64]{1,0:T(8,128)} copy(f32[32,64]{1,0:T(8,128)} %get-tuple-element.14) | data formatting | bytes 16384

commit v2 on v1

--- a/solution.py
+++ b/solution.py
@@ -58,12 +58,12 @@
     sizes,
     img_hbm, txt_hbm, mod_hbm, wqkv_hbm, qg_hbm, kg_hbm, wout_hbm, bout_hbm, stale_hbm,
     fmod_hbm, wfin_hbm, bfin_hbm, lat_hbm, prev_hbm, rowtab_hbm, coltab_hbm,
-    guidance, step_index, step_count,
+    plan_hbm,
     fresh_hbm, next_ref, den_ref,
-    img, txt, mod, wqkv, qg, kg, bout, fmod, wfin, bfin, lat, prev, rowtab, coltab,
-    modded, proj, tabs, fresh, qT, top, total, acc,
-    fl, fr, wbuf, asend, arecv, mixed, final_in, vel, vel_in,
-    in_sem, fresh_sem, ring_send, ring_recv, w_send, w_recv, d_send, d_recv, a_send, a_recv,
+    own, img, txt, mod, wqkv, qg, kg, bout, fmod, wfin, bfin, lat, prev, rowtab, coltab,
+    plan, modded, proj, tabs, fresh, qT, top, total, acc,
+    fl, fr, wbuf, asend, arecv, partial, mixed, final_in, vel, vel_in,
+    own_sem, in_sem, fresh_sem, ring_send, ring_recv, w_send, w_recv, d_send, d_recv, a_send, a_recv,
     v_send, v_recv,
 ):
     n_patch, n_head = sizes
@@ -74,8 +74,7 @@
     right, left = lax.rem(p + 1, n_patch), lax.rem(p + n_patch - 1, n_patch)
     other = 1 - c
     ups = [lax.rem(x + k, n_head) for k in range(n_head)]
-    width = wout_hbm.shape[0]
-    heads = width // HD
+    heads = wout_hbm.shape[0]
     depth = img.shape[1]
     rows = img.shape[0]
     trows = txt.shape[0]
@@ -83,14 +82,24 @@
     out_rows = lat.shape[0]
     inv_root = HD ** (-0.5)
 
+    mine = [
+        pltpu.make_async_copy(
+            stale_hbm.at[kv, :, pl.ds(h * HD, HD)], own.at[h, kv], own_sem.at[h, kv]
+        )
+        for h in range(heads)
+        for kv in range(2)
+    ]
+    for copy in mine:
+        copy.start()
     pairs = [
         (img_hbm, img), (txt_hbm, txt), (mod_hbm, mod),
         (wqkv_hbm.at[0], wqkv.at[0]), (wqkv_hbm.at[1], wqkv.at[1]), (wqkv_hbm.at[2], wqkv.at[2]),
         (rowtab_hbm, rowtab), (coltab_hbm, coltab), (qg_hbm, qg), (kg_hbm, kg),
         (bout_hbm, bout), (fmod_hbm, fmod), (wfin_hbm, wfin), (bfin_hbm, bfin),
         (lat_hbm, lat), (prev_hbm, prev),
-        (wout_hbm.at[:, pl.ds(0, half_w)], wbuf.at[0, pl.ds(0, width)]),
-        (wout_hbm.at[:, pl.ds(half_w, half_w)], wbuf.at[1, pl.ds(0, width)]),
+        (plan_hbm, plan),
+        (wout_hbm.at[:, :, pl.ds(0, half_w)], wbuf.at[0, :, 0]),
+        (wout_hbm.at[:, :, pl.ds(half_w, half_w)], wbuf.at[1, :, 0]),
     ]
     reads = [pltpu.make_async_copy(s, d, in_sem.at[i]) for i, (s, d) in enumerate(pairs)]
     for r in reads:
@@ -102,35 +111,35 @@
         pl.semaphore_signal(barrier, inc=1, device_id=peer, device_id_type=MESH)
     pl.semaphore_wait(barrier, len(peers))
 
-    def hop(side, stage, h, kv):
-        if isinstance(stage, int) and stage == 1:
-            src = stale_hbm.at[kv, :, pl.ds(pl.multiple_of(h * HD, HD), HD)]
-        else:
-            src = (fl, fr)[side].at[stage - 2, h, kv]
-        if isinstance(stage, int) and stage == last:
-            dst = fl.at[stage - 1, h, kv]
-        else:
-            dst = (fl, fr)[side].at[stage - 1, h, kv]
+    def hop(side, stage, h, kv=None):
+        at = (h,) if kv is None else (h, kv)
+        first = isinstance(stage, int) and stage == 1
+        end = isinstance(stage, int) and stage == last
+        src = own.at[at] if first else (fl, fr)[side].at[(stage - 2, *at)]
+        dst = (fl if end else (fl, fr)[side]).at[(stage - 1, *at)]
         return pltpu.make_async_remote_copy(
             src_ref=src, dst_ref=dst,
-            send_sem=ring_send.at[side, stage - 1, h, kv],
-            recv_sem=ring_recv.at[side, stage - 1, h, kv],
+            send_sem=ring_send.at[side, stage - 1, h],
+            recv_sem=ring_recv.at[side, stage - 1, h],
             device_id={"patch": (right, left)[side]}, device_id_type=MESH,
         )
 
-    pieces = [(h, kv) for h in range(heads) for kv in range(2)]
-    cut = len(pieces) // 2
-    final_pieces = (pieces[:cut], pieces[cut:])
-
-    for h, kv in pieces:
+    middle = heads // 2
+    final_pieces = (
+        [(h, None) for h in range(middle)] + [(middle, 0)],
+        [(h, None) for h in range(middle + 1, heads)] + [(middle, 1)],
+    )
+
+    for h in range(heads):
+        mine[2 * h].wait()
+        mine[2 * h + 1].wait()
         for side in range(2):
-            hop(side, 1, h, kv).start()
+            hop(side, 1, h).start()
 
     def forward(stage, h):
-        for kv in range(2):
-            for side in range(2):
-                hop(side, stage, h, kv).wait_recv()
-                hop(side, stage + 1, h, kv).start()
+        for side in range(2):
+            hop(side, stage, h).wait_recv()
+            hop(side, stage + 1, h).start()
 
     def w_copy(i, src, dst, send, recv, dev):
         return pltpu.make_async_remote_copy(
@@ -138,19 +147,18 @@
             device_id=dev, device_id_type=MESH,
         )
 
-    my_cols = wout_hbm.at[:, pl.ds(pl.multiple_of(c * half_w, 128), half_w)]
-    hw = width // 2
-    w1 = w_copy(0, my_cols, wbuf.at[c, pl.ds(width, width)], w_send, w_recv, {"head": ups[1]})
-    w3 = w_copy(1, my_cols, wbuf.at[c, pl.ds(3 * width, width)], w_send, w_recv, {"head": ups[3]})
-    w2a = w_copy(2, wbuf.at[c, pl.ds(width, hw)], wbuf.at[c, pl.ds(2 * width, hw)],
+    my_cols = wout_hbm.at[:, :, pl.ds(pl.multiple_of(c * half_w, 128), half_w)]
+    hd2 = HD // 2
+    w1 = w_copy(0, my_cols, wbuf.at[c, :, 1], w_send, w_recv, {"head": ups[1]})
+    w3 = w_copy(1, my_cols, wbuf.at[c, :, 3], w_send, w_recv, {"head": ups[3]})
+    w2a = w_copy(2, wbuf.at[c, :, 1, pl.ds(0, hd2)], wbuf.at[c, :, 2, pl.ds(0, hd2)],
                  w_send, w_recv, {"head": ups[1]})
-    w2b = w_copy(3, wbuf.at[c, pl.ds(3 * width + hw, hw)], wbuf.at[c, pl.ds(2 * width + hw, hw)],
+    w2b = w_copy(3, wbuf.at[c, :, 3, pl.ds(hd2, hd2)], wbuf.at[c, :, 2, pl.ds(hd2, hd2)],
                  w_send, w_recv, {"head": ups[3]})
-    d_out = [w_copy(k - 1, wbuf.at[c, pl.ds(k * width, width)], wbuf.at[c, pl.ds(k * width, width)],
-                    d_send, d_recv, {"cfg": other}) for k in range(1, n_head)]
-    d_in = [w_copy(k - 1, wbuf.at[other, pl.ds(k * width, width)],
-                   wbuf.at[other, pl.ds(k * width, width)],
-                   d_send, d_recv, {"cfg": other}) for k in range(1, n_head)]
+    d_out = [w_copy(k - 1, wbuf.at[c, :, k], wbuf.at[c, :, k], d_send, d_recv, {"cfg": other})
+             for k in range(1, n_head)]
+    d_in = [w_copy(k - 1, wbuf.at[other, :, k], wbuf.at[other, :, k], d_send, d_recv,
+                   {"cfg": other}) for k in range(1, n_head)]
     w1.start()
     w3.start()
 
@@ -259,12 +267,12 @@
     lax.fori_loop(relay, last - 2, step, 0)
 
     for h in range(heads):
-        for kv in range(2):
-            for side in range(2):
-                hop(side, last - 1, h, kv).wait_recv()
-                if (h, kv) in final_pieces[side]:
-                    hop(side, last, h, kv).start()
+        for side in range(2):
+            hop(side, last - 1, h).wait_recv()
         both(last - 2, h)
+    for side in range(2):
+        for h, kv in final_pieces[side]:
+            hop(side, last, h, kv).start()
 
     w2a.wait_recv()
     w2b.wait_recv()
@@ -280,45 +288,59 @@
     for copy in d_in:
         copy.wait_recv()
 
-    for h in range(heads):
-        for kv in range(2):
-            for side in range(2):
-                if (h, kv) in final_pieces[side]:
-                    hop(side, last, h, kv).wait_recv()
+    def a_copy(h, k):
+        return pltpu.make_async_remote_copy(
+            src_ref=asend.at[h, ups[k]], dst_ref=arecv.at[h, :, pl.ds(k * HD, HD)],
+            send_sem=a_send.at[h, k - 1], recv_sem=a_recv.at[h, k - 1],
+            device_id={"head": ups[k]}, device_id_type=MESH,
+        )
+
+    def end_of(h):
+        for side in range(2):
+            for at in final_pieces[side]:
+                if at[0] == h:
+                    hop(side, last, *at).wait_recv()
         attend(h, fl[last - 1, h, 0], fl[last - 1, h, 1])
         out = (acc[h] / total[h]).astype(BF).T
         for part in range(2):
             for k in range(n_head):
                 at = part * n_head * out_rows + k * out_rows
-                asend[k, pl.ds(part * out_rows, out_rows), pl.ds(h * HD, HD)] = (
-                    out[at : at + out_rows, :]
-                )
-
-    a_copies = [
-        pltpu.make_async_remote_copy(
-            src_ref=asend.at[ups[k]], dst_ref=arecv.at[:, pl.ds(k * width, width)],
-            send_sem=a_send.at[k - 1], recv_sem=a_recv.at[k - 1],
-            device_id={"head": ups[k]}, device_id_type=MESH,
-        )
-        for k in range(1, n_head)
-    ]
-    for k in (2, 1, 3):
-        a_copies[k - 1].start()
-    arecv[:, pl.ds(0, width)] = asend[x]
-    for copy in a_copies:
-        copy.wait_recv()
+                asend[h, k, pl.ds(part * out_rows, out_rows), :] = out[at : at + out_rows, :]
+        for k in (2, 1, 3):
+            a_copy(h, k).start()
+        arecv[h, :, pl.ds(0, HD)] = asend[h, x]
+
+    early = [h for h in range(heads) if h != middle]
+    for h in early:
+        end_of(h)
+    end_of(middle)
 
     chunk = 512
-    attn = arecv[...]
+    for h in early:
+        for k in range(1, n_head):
+            a_copy(h, k).wait_recv()
     for n in range(depth // chunk):
         half, at = divmod(n * chunk, half_w)
         cols = pl.ds(n * chunk, chunk)
-        projected = jnp.dot(attn, wbuf[half, :, pl.ds(at, chunk)], preferred_element_type=F32)
+        sums = bout[:, cols]
+        for h in early:
+            w = wbuf[half, h, :, :, pl.ds(at, chunk)].reshape(n_head * HD, chunk)
+            sums = sums + jnp.dot(arecv[h], w, preferred_element_type=F32)
+        partial[:, cols] = sums
+    for k in range(1, n_head):
+        a_copy(middle, k).wait_recv()
+    for n in range(depth // chunk):
+        half, at = divmod(n * chunk, half_w)
+        cols = pl.ds(n * chunk, chunk)
+        w = wbuf[half, middle, :, :, pl.ds(at, chunk)].reshape(n_head * HD, chunk)
+        projected = partial[:, cols] + jnp.dot(arecv[middle], w, preferred_element_type=F32)
         for part in range(2):
-            own = pl.ds(pl.multiple_of(part * n_head * out_rows + x * out_rows, out_rows), out_rows)
-            mixed[pl.ds(part * out_rows, out_rows), cols] = img[own, cols].astype(F32) + mod[
+            rows_of = pl.ds(
+                pl.multiple_of(part * n_head * out_rows + x * out_rows, out_rows), out_rows
+            )
+            mixed[pl.ds(part * out_rows, out_rows), cols] = img[rows_of, cols].astype(F32) + mod[
                 2, :, cols
-            ] * (projected[part * out_rows : (part + 1) * out_rows] + bout[:, cols])
+            ] * projected[part * out_rows : (part + 1) * out_rows]
 
     def finish(i, carry):
         at = pl.multiple_of(i * block, block)
@@ -344,9 +366,7 @@
     )
     swap.start()
 
-    index = jnp.full((1, ch), step_index[0], jnp.int32).astype(F32)
-    count = jnp.full((1, ch), step_count[0], jnp.int32).astype(F32)
-    scale = jnp.full((1, ch), guidance[0], F32)
+    index, count, scale = (plan[i : i + 1, pl.ds(0, ch)] for i in range(3))
     sigma_prev = noise_level(index - 1.0, count)
     sigma_now = noise_level(index, count)
     sigma_next = noise_level(index + 1.0, count)
@@ -354,10 +374,10 @@
     step_prev = log_ratio(sigma_now) - log_ratio(sigma_prev)
     ratio = step_prev / step_now
     swap.wait_recv()
-    mine = vel[c, :, pl.ds(0, ch)]
+    ours = vel[c, :, pl.ds(0, ch)]
     theirs = vel_in[:, pl.ds(0, ch)]
-    cond = jnp.where(c == 0, mine, theirs)
-    uncond = jnp.where(c == 0, theirs, mine)
+    cond = jnp.where(c == 0, ours, theirs)
+    uncond = jnp.where(c == 0, theirs, ours)
     guided = uncond + scale * (cond - uncond)
     denoised = lat[...] - sigma_now * guided
     blend = (1.0 + 0.5 / ratio) * denoised - 0.5 / ratio * prev[...]
@@ -367,22 +387,39 @@
     den_ref[...] = denoised
 
     fresh_out.wait()
-    for h, kv in pieces:
+    for h in range(heads):
         for side in range(2):
-            hop(side, 1, h, kv).wait_send()
+            hop(side, 1, h).wait_send()
 
     def drain(stage, carry):
-        for h, kv in pieces:
+        for h in range(heads):
             for side in range(2):
-                hop(side, stage, h, kv).wait_send()
+                hop(side, stage, h).wait_send()
         return carry
 
     lax.fori_loop(2, last, drain, 0)
     for side in range(2):
         for h, kv in final_pieces[side]:
             hop(side, last, h, kv).wait_send()
-    for copy in (w1, w3, w2a, w2b, *d_out, *a_copies, swap):
+    for h in range(heads):
+        for k in range(1, n_head):
+            a_copy(h, k).wait_send()
+    for copy in (w1, w3, w2a, w2b, *d_out, swap):
         copy.wait_send()
+
+
+def hand_over(*refs):
+    n = 3
+    ins, outs, held, sems = refs[:n], refs[n : 2 * n], refs[2 * n : 3 * n], refs[3 * n :]
+    reads = [pltpu.make_async_copy(a, b, sems[0].at[i]) for i, (a, b) in enumerate(zip(ins, held))]
+    writes = [pltpu.make_async_copy(a, b, sems[1].at[i]) for i, (a, b) in enumerate(zip(held, outs))]
+    for copy in reads:
+        copy.start()
+    for i in range(n):
+        reads[i].wait()
+        writes[i].start()
+    for copy in writes:
+        copy.wait()
 
 
 def body(
@@ -400,8 +437,11 @@
     last = n_patch // 2
     n_rows = n_patch * rows // GRID_W
     rowtab, coltab = rotation_tables(n_rows)
+    row = lax.broadcasted_iota(jnp.int32, (8, 128), 0)
+    plan = jnp.where(
+        row == 0, step_index.astype(F32), jnp.where(row == 1, step_count.astype(F32), guidance)
+    )
     any_spec = pl.BlockSpec(memory_space=pl.ANY)
-    smem = pl.BlockSpec(memory_space=pltpu.SMEM)
     vmem = pl.BlockSpec(memory_space=pltpu.VMEM)
     dma = pltpu.SemaphoreType.DMA
     V = pltpu.VMEM
@@ -412,35 +452,44 @@
             jax.ShapeDtypeStruct((out_rows, ch), F32),
             jax.ShapeDtypeStruct((out_rows, ch), F32),
         ),
-        in_specs=[any_spec] * 16 + [smem] * 3,
+        in_specs=[any_spec] * 17,
         out_specs=(any_spec, vmem, vmem),
         scratch_shapes=[
-            V((rows, depth), BF), V((trows, depth), BF), V((3, 1, depth), F32),
+            V((heads, 2, kv_rows, HD), BF), V((rows, depth), BF), V((trows, depth), BF), V((3, 1, depth), F32),
             V((3, depth, width), BF), V((1, HD), F32), V((1, HD), F32), V((1, depth), F32),
             V((2, depth), F32), V((ch, depth), BF), V((1, ch), F32), V((out_rows, ch), F32),
             V((out_rows, ch), F32), V((3, n_rows, HD), F32), V((3, GRID_W, HD), F32),
+            V((8, 128), F32),
             V((kv_rows, depth), BF), V((3, kv_rows, width), F32), V((3, kv_rows, HD), F32),
             V((2, kv_rows, width), BF), V((heads, HD, rows), BF), V((heads, 1, rows), F32),
             V((heads, 1, rows), F32), V((heads, HD, rows), F32),
             V((last, heads, 2, kv_rows, HD), BF), V((last - 1, heads, 2, kv_rows, HD), BF),
-            V((2, n_head * width, depth // 2), BF),
-            V((n_head, 2 * out_rows, width), BF), V((2 * out_rows, n_head * width), BF),
-            V((2 * out_rows, depth), F32), V((2 * out_rows, depth), BF),
+            V((2, heads, n_head, HD, depth // 2), BF),
+            V((heads, n_head, 2 * out_rows, HD), BF), V((heads, 2 * out_rows, n_head * HD), BF),
+            V((2 * out_rows, depth), F32), V((2 * out_rows, depth), F32),
+            V((2 * out_rows, depth), BF),
             V((2, out_rows, 128), F32), V((out_rows, 128), F32),
-            dma((18,)), dma((1,)),
-            dma((2, last, heads, 2)), dma((2, last, heads, 2)),
+            dma((heads, 2)), dma((19,)), dma((1,)),
+            dma((2, last, heads)), dma((2, last, heads)),
             dma((4,)), dma((4,)), dma((n_head - 1,)), dma((n_head - 1,)),
-            dma((n_head - 1,)), dma((n_head - 1,)), dma((1,)), dma((1,)),
+            dma((heads, n_head - 1)), dma((heads, n_head - 1)), dma((1,)), dma((1,)),
         ],
         compiler_params=pltpu.CompilerParams(
             collective_id=0, has_side_effects=True, vmem_limit_bytes=60 * 1024 * 1024
         ),
     )(
         img_hidden[0], txt_hidden[0], modulation.transpose(1, 0, 2), w_qkv.transpose(1, 0, 2),
-        q_gain[None], k_gain[None], w_out, b_out[None], stale_kv[0], final_mod[0], w_final.T,
+        q_gain[None], k_gain[None], w_out.reshape(heads, HD, depth), b_out[None], stale_kv[0], final_mod[0], w_final.T,
         b_final[None], latent, prev_denoised, jnp.asarray(rowtab), jnp.asarray(coltab),
-        guidance, step_index, step_count,
-    )
+        plan,
+    )
+    outs = pl.pallas_call(
+        hand_over,
+        out_shape=tuple(jax.ShapeDtypeStruct(o.shape, o.dtype) for o in outs),
+        in_specs=[any_spec] * 3,
+        out_specs=(any_spec,) * 3,
+        scratch_shapes=[V(o.shape, o.dtype) for o in outs] + [dma((3,)), dma((3,))],
+    )(*outs)
     return outs[0][None], outs[1], outs[2]
 
 

time: 115 us -> 113 us (0.983)
  local copies, waits for them, and re-layouts: 4.45 us -> 0 us
  Pallas kernels: 107 us -> 110 us
    unnamed x3 -> x0, local copies, waits for them, and re-layouts: 4.45 us -> none
    pallas_call x0 -> x1, Pallas kernels: none -> 1.81 us  [body(): pl.pallas_call(hand_over, out_shape=tuple((jax.ShapeDtypeStruct(o.shape,...]
where the time goes in v2:
time: 113 us
  Pallas kernels  110 us (97%)
  between operations  2.59 us (2%)
    pallas_call x1, Pallas kernels, body(): pl.pallas_call(functools.partial(kernel, sizes), out_shape=(jax.ShapeDtyp...  108 us

profile of v2, /device:TPU:33, one launch (start us, length us, event | category | flops | bytes accessed | tf_op | source)
XLA Modules:
  0.0 112.8 jit_solution(12677108105104659558)
XLA Ops:
  2.6 0.7 broadcast_select_fusion.plan_hbm
  3.3 107.7 %shard_map.205 = (bf16[2,272,384]{2,1,0:T(8,128)(2,1)}, f32[32,64]{1,0:T(8,128)}, f32[32,64]{1,0:T(8,128)}) custom-call(bf16[256,3072]{1,0:T(8,128)(2,1)} %bitcast.19, bf16[16,3072]{1,0:T(8,128)(2,1)} %bitcast.22, f32[3,1,3072]{2,1,0:T(1,128)} %bitcast.23, bf16[3,3072,384]{2,1,0:T(8,128)(2,1)} %bitcast.17, f32[1,128]{1,0:T(1,128)} %bitcast.26, ...), custom_call_target="tpu_custom_call" | custom-call | tf_op jit(solution)/shard_map/pallas_call | solution.py:448
  111.0 1.8 %shard_map.206 = (bf16[2,272,384]{2,1,0:T(8,128)(2,1)}, f32[32,64]{1,0:T(8,128)}, f32[32,64]{1,0:T(8,128)}) custom-call(bf16[2,272,384]{2,1,0:T(8,128)(2,1)} %get-tuple-element.9.refs_0_, f32[32,64]{1,0:T(8,128)} %get-tuple-element.10.refs_1_, f32[32,64]{1,0:T(8,128)} %get-tuple-element.11.refs_2_), custom_call_target="tpu_custom_call" | custom-call | tf_op jit(solution)/shard_map/pallas_call | solution.py:486
  (2 shorter events, 0.0 us)

commit v3 on v2

--- a/solution.py
+++ b/solution.py
@@ -58,11 +58,11 @@
     sizes,
     img_hbm, txt_hbm, mod_hbm, wqkv_hbm, qg_hbm, kg_hbm, wout_hbm, bout_hbm, stale_hbm,
     fmod_hbm, wfin_hbm, bfin_hbm, lat_hbm, prev_hbm, rowtab_hbm, coltab_hbm,
-    plan_hbm,
+    guidance_hbm, index_hbm, count_hbm,
     fresh_hbm, next_ref, den_ref,
     own, img, txt, mod, wqkv, qg, kg, bout, fmod, wfin, bfin, lat, prev, rowtab, coltab,
-    plan, modded, proj, tabs, fresh, qT, top, total, acc,
-    fl, fr, wbuf, asend, arecv, partial, mixed, final_in, vel, vel_in,
+    guidance, step_index, step_count, modded, proj, tabs, fresh, qT, top, total, acc,
+    fl, fr, wbuf, asend, arecv, partial, mixed, vel, vel_in,
     own_sem, in_sem, fresh_sem, ring_send, ring_recv, w_send, w_recv, d_send, d_recv, a_send, a_recv,
     v_send, v_recv,
 ):
@@ -75,6 +75,7 @@
     other = 1 - c
     ups = [lax.rem(x + k, n_head) for k in range(n_head)]
     heads = wout_hbm.shape[0]
+    assert heads == 3
     depth = img.shape[1]
     rows = img.shape[0]
     trows = txt.shape[0]
@@ -97,7 +98,7 @@
         (rowtab_hbm, rowtab), (coltab_hbm, coltab), (qg_hbm, qg), (kg_hbm, kg),
         (bout_hbm, bout), (fmod_hbm, fmod), (wfin_hbm, wfin), (bfin_hbm, bfin),
         (lat_hbm, lat), (prev_hbm, prev),
-        (plan_hbm, plan),
+        (guidance_hbm, guidance), (index_hbm, step_index), (count_hbm, step_count),
         (wout_hbm.at[:, :, pl.ds(0, half_w)], wbuf.at[0, :, 0]),
         (wout_hbm.at[:, :, pl.ds(half_w, half_w)], wbuf.at[1, :, 0]),
     ]
@@ -130,16 +131,19 @@
         [(h, None) for h in range(middle + 1, heads)] + [(middle, 1)],
     )
 
-    for h in range(heads):
-        mine[2 * h].wait()
-        mine[2 * h + 1].wait()
+    def turn_of(side, i):
+        return i if side == 0 else heads - 1 - i
+
+    for copy in mine:
+        copy.wait()
+    for i in range(heads):
         for side in range(2):
-            hop(side, 1, h).start()
-
-    def forward(stage, h):
+            hop(side, 1, turn_of(side, i)).start()
+
+    def forward(stage, i):
         for side in range(2):
-            hop(side, stage, h).wait_recv()
-            hop(side, stage + 1, h).start()
+            hop(side, stage, turn_of(side, i)).wait_recv()
+            hop(side, stage + 1, turn_of(side, i)).start()
 
     def w_copy(i, src, dst, send, recv, dev):
         return pltpu.make_async_remote_copy(
@@ -182,15 +186,10 @@
     def project(j, carry):
         pltpu.make_async_copy(wqkv_hbm.at[j], wqkv.at[j], in_sem.at[3 + j]).wait()
         proj[j] = jnp.dot(modded[...], wqkv[j], preferred_element_type=F32)
-        return carry
-
-    for j in range(3):
-        project(j, 0)
-        if j < heads:
-            forward(1, j)
-    for h in range(3, heads):
-        forward(1, h)
-
+        forward(1, j)
+        return carry
+
+    lax.fori_loop(0, heads, project, 0)
     for r in reads[6:10]:
         r.wait()
 
@@ -215,11 +214,14 @@
             + pltpu.roll(scaled, quarter, 1) * tabs[2, pl.ds(first, n), :]
         )
 
-    for h in range(heads):
-        cols = pl.ds(h * HD, HD)
+    def turn(h, carry):
+        cols = pl.ds(pl.multiple_of(h * HD, HD), HD)
         q = turned(proj[0, pl.ds(trows, rows), cols], qg[...], trows).astype(BF)
         qT[h] = q.T
         fresh[0, :, cols] = turned(proj[1, :, cols], kg[...], 0).astype(BF)
+        return carry
+
+    lax.fori_loop(0, heads, turn, 0)
     fresh[1] = proj[2].astype(BF)
     fresh_out = pltpu.make_async_copy(fresh, fresh_hbm, fresh_sem.at[0])
     fresh_out.start()
@@ -240,40 +242,53 @@
             vals, expo.astype(BF), (((0,), (0,)), ((), ())), preferred_element_type=F32
         )
 
-    for h in range(heads):
-        cols = pl.ds(h * HD, HD)
+    def nearest(h, carry):
+        cols = pl.ds(pl.multiple_of(h * HD, HD), HD)
         attend(h, fresh[0, :, cols], fresh[1, :, cols])
-
-    def both(stage, h):
-        attend(h, fl[stage - 1, h, 0], fl[stage - 1, h, 1])
-        attend(h, fr[stage - 1, h, 0], fr[stage - 1, h, 1])
-
-    def step(stage, carry):
-        def one(h, inner):
-            forward(stage + 1, h)
-            both(stage, h)
-            return inner
-
-        return lax.fori_loop(0, heads, one, carry)
-
-    relay = (last - 2) // 2 + 1
-    lax.fori_loop(1, relay, step, 0)
-    w1.wait_recv()
-    w2a.start()
-    d_out[0].start()
-    w3.wait_recv()
-    w2b.start()
-    d_out[2].start()
-    lax.fori_loop(relay, last - 2, step, 0)
-
-    for h in range(heads):
+        return carry
+
+    lax.fori_loop(0, heads, nearest, 0)
+
+    def both(stage, i):
+        for side, buffer in enumerate((fl, fr)):
+            h = turn_of(side, i)
+            attend(h, buffer[stage - 1, h, 0], buffer[stage - 1, h, 1])
+
+    relay = (last - 2) // 2
+
+    def step(i, carry):
+        stage, j = i // heads + 1, lax.rem(i, heads)
         for side in range(2):
-            hop(side, last - 1, h).wait_recv()
-        both(last - 2, h)
-    for side in range(2):
-        for h, kv in final_pieces[side]:
-            hop(side, last, h, kv).start()
-
+            hop(side, stage + 1, turn_of(side, j)).wait_recv()
+
+        @pl.when(stage < last - 2)
+        def _():
+            for side in range(2):
+                hop(side, stage + 2, turn_of(side, j)).start()
+
+        @pl.when(jnp.logical_and(stage == last - 2, j < middle))
+        def _():
+            for side in range(2):
+                hop(side, last, turn_of(side, j)).start()
+
+        @pl.when(jnp.logical_and(stage == last - 2, j == middle))
+        def _():
+            for side in range(2):
+                hop(side, last, middle, side).start()
+
+        @pl.when(i == (relay - 1) * heads)
+        def _():
+            w1.wait_recv()
+            w2a.start()
+            d_out[0].start()
+            w3.wait_recv()
+            w2b.start()
+            d_out[2].start()
+
+        both(stage, j)
+        return carry
+
+    lax.fori_loop(0, (last - 2) * heads, step, 0)
     w2a.wait_recv()
     w2b.wait_recv()
     d_out[1].start()
@@ -295,11 +310,17 @@
             device_id={"head": ups[k]}, device_id_type=MESH,
         )
 
-    def end_of(h):
-        for side in range(2):
-            for at in final_pieces[side]:
-                if at[0] == h:
-                    hop(side, last, *at).wait_recv()
+    def end_of(i, carry):
+        h = lax.rem(2 * i, heads)
+        for j in range(heads):
+
+            @pl.when(i == j)
+            def _(j=j):
+                for side in range(2):
+                    for at in final_pieces[side]:
+                        if at[0] == 2 * j % heads:
+                            hop(side, last, *at).wait_recv()
+
         attend(h, fl[last - 1, h, 0], fl[last - 1, h, 1])
         out = (acc[h] / total[h]).astype(BF).T
         for part in range(2):
@@ -309,31 +330,40 @@
         for k in (2, 1, 3):
             a_copy(h, k).start()
         arecv[h, :, pl.ds(0, HD)] = asend[h, x]
-
+        return carry
+
+    lax.fori_loop(0, heads, end_of, 0)
+
+    chunk = 512
     early = [h for h in range(heads) if h != middle]
-    for h in early:
-        end_of(h)
-    end_of(middle)
-
-    chunk = 512
     for h in early:
         for k in range(1, n_head):
             a_copy(h, k).wait_recv()
-    for n in range(depth // chunk):
-        half, at = divmod(n * chunk, half_w)
-        cols = pl.ds(n * chunk, chunk)
+
+    def chunk_of(n):
+        per_half = half_w // chunk
+        at = pl.multiple_of(lax.rem(n, per_half) * chunk, chunk)
+        return n // per_half, pl.ds(at, chunk), pl.ds(pl.multiple_of(n * chunk, chunk), chunk)
+
+    def product(h, half, at):
+        w = wbuf[half, h, :, :, at].reshape(n_head * HD, chunk)
+        return jnp.dot(arecv[h], w, preferred_element_type=F32)
+
+    def first_heads(n, carry):
+        half, at, cols = chunk_of(n)
         sums = bout[:, cols]
         for h in early:
-            w = wbuf[half, h, :, :, pl.ds(at, chunk)].reshape(n_head * HD, chunk)
-            sums = sums + jnp.dot(arecv[h], w, preferred_element_type=F32)
+            sums = sums + product(h, half, at)
         partial[:, cols] = sums
+        return carry
+
+    lax.fori_loop(0, depth // chunk, first_heads, 0)
     for k in range(1, n_head):
         a_copy(middle, k).wait_recv()
-    for n in range(depth // chunk):
-        half, at = divmod(n * chunk, half_w)
-        cols = pl.ds(n * chunk, chunk)
-        w = wbuf[half, middle, :, :, pl.ds(at, chunk)].reshape(n_head * HD, chunk)
-        projected = partial[:, cols] + jnp.dot(arecv[middle], w, preferred_element_type=F32)
+
+    def last_head(n, carry):
+        half, at, cols = chunk_of(n)
+        projected = partial[:, cols] + product(middle, half, at)
         for part in range(2):
             rows_of = pl.ds(
                 pl.multiple_of(part * n_head * out_rows + x * out_rows, out_rows), out_rows
@@ -341,21 +371,26 @@
             mixed[pl.ds(part * out_rows, out_rows), cols] = img[rows_of, cols].astype(F32) + mod[
                 2, :, cols
             ] * projected[part * out_rows : (part + 1) * out_rows]
-
-    def finish(i, carry):
-        at = pl.multiple_of(i * block, block)
-        final_in[pl.ds(at, block), :] = (
-            normed(mixed[pl.ds(at, block), :]) * (1.0 + fmod[1:2, :]) + fmod[0:1, :]
-        ).astype(BF)
-        return carry
-
-    lax.fori_loop(0, 2 * out_rows // block, finish, 0)
-    velocity = (
-        lax.dot_general(
-            final_in[...], wfin[...], (((1,), (1,)), ((), ())), preferred_element_type=F32
-        )
-        + bfin[...]
-    )
+        values = mixed[:, cols]
+        for at in range(0, chunk, HD):
+            carry = carry + values[:, at : at + HD]
+        return carry
+
+    sums = lax.fori_loop(0, depth // chunk, last_head, jnp.zeros((2 * out_rows, HD), F32))
+
+    mean = jnp.sum(sums, axis=-1, keepdims=True) * (1.0 / depth)
+    squares = jnp.zeros((2 * out_rows, HD), F32)
+    for at in range(0, depth, HD):
+        centered = mixed[:, pl.ds(at, HD)] - mean
+        squares = squares + centered * centered
+    scale = lax.rsqrt(jnp.sum(squares, axis=-1, keepdims=True) * (1.0 / depth) + EPS)
+    velocity = bfin[...]
+    for at in range(0, depth, chunk):
+        cols = pl.ds(at, chunk)
+        final_in = ((mixed[:, cols] - mean) * scale * (1.0 + fmod[1:2, cols]) + fmod[0:1, cols]).astype(BF)
+        velocity = velocity + lax.dot_general(
+            final_in, wfin[:, cols], (((1,), (1,)), ((), ())), preferred_element_type=F32
+        )
     ch = velocity.shape[1]
     vel[...] = jnp.zeros(vel.shape, F32)
     vel[0, :, pl.ds(0, ch)] = velocity[:out_rows]
@@ -366,7 +401,9 @@
     )
     swap.start()
 
-    index, count, scale = (plan[i : i + 1, pl.ds(0, ch)] for i in range(3))
+    index = jnp.full((1, ch), step_index[0], jnp.int32).astype(F32)
+    count = jnp.full((1, ch), step_count[0], jnp.int32).astype(F32)
+    strength = jnp.full((1, ch), guidance[0], F32)
     sigma_prev = noise_level(index - 1.0, count)
     sigma_now = noise_level(index, count)
     sigma_next = noise_level(index + 1.0, count)
@@ -378,7 +415,7 @@
     theirs = vel_in[:, pl.ds(0, ch)]
     cond = jnp.where(c == 0, ours, theirs)
     uncond = jnp.where(c == 0, theirs, ours)
-    guided = uncond + scale * (cond - uncond)
+    guided = uncond + strength * (cond - uncond)
     denoised = lat[...] - sigma_now * guided
     blend = (1.0 + 0.5 / ratio) * denoised - 0.5 / ratio * prev[...]
     next_ref[...] = (
@@ -437,10 +474,6 @@
     last = n_patch // 2
     n_rows = n_patch * rows // GRID_W
     rowtab, coltab = rotation_tables(n_rows)
-    row = lax.broadcasted_iota(jnp.int32, (8, 128), 0)
-    plan = jnp.where(
-        row == 0, step_index.astype(F32), jnp.where(row == 1, step_count.astype(F32), guidance)
-    )
     any_spec = pl.BlockSpec(memory_space=pl.ANY)
     vmem = pl.BlockSpec(memory_space=pltpu.VMEM)
     dma = pltpu.SemaphoreType.DMA
@@ -452,14 +485,14 @@
             jax.ShapeDtypeStruct((out_rows, ch), F32),
             jax.ShapeDtypeStruct((out_rows, ch), F32),
         ),
-        in_specs=[any_spec] * 17,
+        in_specs=[any_spec] * 16 + [pl.BlockSpec(memory_space=pltpu.HBM)] * 3,
         out_specs=(any_spec, vmem, vmem),
         scratch_shapes=[
             V((heads, 2, kv_rows, HD), BF), V((rows, depth), BF), V((trows, depth), BF), V((3, 1, depth), F32),
             V((3, depth, width), BF), V((1, HD), F32), V((1, HD), F32), V((1, depth), F32),
             V((2, depth), F32), V((ch, depth), BF), V((1, ch), F32), V((out_rows, ch), F32),
             V((out_rows, ch), F32), V((3, n_rows, HD), F32), V((3, GRID_W, HD), F32),
-            V((8, 128), F32),
+            pltpu.SMEM((1,), F32), pltpu.SMEM((1,), jnp.int32), pltpu.SMEM((1,), jnp.int32),
             V((kv_rows, depth), BF), V((3, kv_rows, width), F32), V((3, kv_rows, HD), F32),
             V((2, kv_rows, width), BF), V((heads, HD, rows), BF), V((heads, 1, rows), F32),
             V((heads, 1, rows), F32), V((heads, HD, rows), F32),
@@ -467,9 +500,8 @@
             V((2, heads, n_head, HD, depth // 2), BF),
             V((heads, n_head, 2 * out_rows, HD), BF), V((heads, 2 * out_rows, n_head * HD), BF),
             V((2 * out_rows, depth), F32), V((2 * out_rows, depth), F32),
-            V((2 * out_rows, depth), BF),
             V((2, out_rows, 128), F32), V((out_rows, 128), F32),
-            dma((heads, 2)), dma((19,)), dma((1,)),
+            dma((heads, 2)), dma((21,)), dma((1,)),
             dma((2, last, heads)), dma((2, last, heads)),
             dma((4,)), dma((4,)), dma((n_head - 1,)), dma((n_head - 1,)),
             dma((heads, n_head - 1)), dma((heads, n_head - 1)), dma((1,)), dma((1,)),
@@ -481,7 +513,7 @@
         img_hidden[0], txt_hidden[0], modulation.transpose(1, 0, 2), w_qkv.transpose(1, 0, 2),
         q_gain[None], k_gain[None], w_out.reshape(heads, HD, depth), b_out[None], stale_kv[0], final_mod[0], w_final.T,
         b_final[None], latent, prev_denoised, jnp.asarray(rowtab), jnp.asarray(coltab),
-        plan,
+        guidance, step_index, step_count,
     )
     outs = pl.pallas_call(
         hand_over,

time: 113 us -> 113 us (level)
  no operation moved by 1% of the time
where the time goes in v3:
time: 113 us; the launch traced here: 112 us
  Pallas kernels  110 us (97%)
  between operations  2.58 us (2%)
    pallas_call x1, Pallas kernels, body(): pl.pallas_call(functools.partial(kernel, sizes), out_shape=(jax.ShapeDtyp...  108 us

profile of v3, /device:TPU:33, one launch (start us, length us, event | category | flops | bytes accessed | tf_op | source)
XLA Modules:
  0.0 112.5 jit_solution(11067377035031223835)
XLA Ops:
  2.6 108.1 %shard_map.202 = (bf16[2,272,384]{2,1,0:T(8,128)(2,1)}, f32[32,64]{1,0:T(8,128)}, f32[32,64]{1,0:T(8,128)}) custom-call(bf16[256,3072]{1,0:T(8,128)(2,1)} %bitcast.15, bf16[16,3072]{1,0:T(8,128)(2,1)} %bitcast.18, f32[3,1,3072]{2,1,0:T(1,128)} %bitcast.19, bf16[3,3072,384]{2,1,0:T(8,128)(2,1)} %bitcast.13, f32[1,128]{1,0:T(1,128)} %bitcast.22, ...), custom_call_target="tpu_custom_call" | custom-call | tf_op jit(solution)/shard_map/pallas_call | solution.py:481
  110.6 1.8 %shard_map.203 = (bf16[2,272,384]{2,1,0:T(8,128)(2,1)}, f32[32,64]{1,0:T(8,128)}, f32[32,64]{1,0:T(8,128)}) custom-call(bf16[2,272,384]{2,1,0:T(8,128)(2,1)} %get-tuple-element.9.refs_0_, f32[32,64]{1,0:T(8,128)} %get-tuple-element.10.refs_1_, f32[32,64]{1,0:T(8,128)} %get-tuple-element.11.refs_2_), custom_call_target="tpu_custom_call" | custom-call | tf_op jit(solution)/shard_map/pallas_call | solution.py:518

commit v4 on v3

--- a/solution.py
+++ b/solution.py
@@ -62,9 +62,9 @@
     fresh_hbm, next_ref, den_ref,
     own, img, txt, mod, wqkv, qg, kg, bout, fmod, wfin, bfin, lat, prev, rowtab, coltab,
     guidance, step_index, step_count, modded, proj, tabs, fresh, qT, top, total, acc,
-    fl, fr, wbuf, asend, arecv, partial, mixed, vel, vel_in,
+    fl, fr, wbuf, asend, arecv, partial, mixed, hid_in, gate_in, fmod_in,
     own_sem, in_sem, fresh_sem, ring_send, ring_recv, w_send, w_recv, d_send, d_recv, a_send, a_recv,
-    v_send, v_recv,
+    b_send, b_recv,
 ):
     n_patch, n_head = sizes
     last = n_patch // 2
@@ -107,7 +107,8 @@
         r.start()
 
     barrier = pltpu.get_barrier_semaphore()
-    peers = [{"patch": right}, {"patch": left}, {"cfg": other}] + [{"head": u} for u in ups[1:]]
+    peers = [{"patch": right}, {"patch": left}, {"cfg": other}]
+    peers += [{"head": u, "cfg": f} for u in ups[1:] for f in (c, other)]
     for peer in peers:
         pl.semaphore_signal(barrier, inc=1, device_id=peer, device_id_type=MESH)
     pl.semaphore_wait(barrier, len(peers))
@@ -166,6 +167,20 @@
     w1.start()
     w3.start()
 
+    def latent_rows(part):
+        at = part * n_head * out_rows + x * out_rows
+        return pl.ds(pl.multiple_of(at, out_rows), out_rows)
+
+    b_copies = [
+        w_copy(i, src, dst, b_send, b_recv, {"cfg": other})
+        for i, (src, dst) in enumerate([
+            (img_hbm.at[latent_rows(other)], hid_in), (mod_hbm.at[2], gate_in),
+            (fmod_hbm, fmod_in),
+        ])
+    ]
+    for copy in b_copies:
+        copy.start()
+
     for r in reads[:3]:
         r.wait()
     block = 16
@@ -303,11 +318,16 @@
     for copy in d_in:
         copy.wait_recv()
 
-    def a_copy(h, k):
+    sides = (c, other)
+    peers8 = [(f, k) for k in (2, 1, 3, 0) for f in range(2) if (f, k) != (0, 0)]
+
+    def a_copy(h, f, k):
+        dev = {"head": ups[k], "cfg": sides[f]}
         return pltpu.make_async_remote_copy(
-            src_ref=asend.at[h, ups[k]], dst_ref=arecv.at[h, :, pl.ds(k * HD, HD)],
-            send_sem=a_send.at[h, k - 1], recv_sem=a_recv.at[h, k - 1],
-            device_id={"head": ups[k]}, device_id_type=MESH,
+            src_ref=asend.at[h, sides[f], ups[k]],
+            dst_ref=arecv.at[h, f, :, pl.ds(k * HD, HD)],
+            send_sem=a_send.at[h, f, k], recv_sem=a_recv.at[h, f, k],
+            device_id=dev, device_id_type=MESH,
         )
 
     def end_of(i, carry):
@@ -326,10 +346,10 @@
         for part in range(2):
             for k in range(n_head):
                 at = part * n_head * out_rows + k * out_rows
-                asend[h, k, pl.ds(part * out_rows, out_rows), :] = out[at : at + out_rows, :]
-        for k in (2, 1, 3):
-            a_copy(h, k).start()
-        arecv[h, :, pl.ds(0, HD)] = asend[h, x]
+                asend[h, part, k] = out[at : at + out_rows, :]
+        for f, k in peers8:
+            a_copy(h, f, k).start()
+        arecv[h, 0, :, pl.ds(0, HD)] = asend[h, c, x]
         return carry
 
     lax.fori_loop(0, heads, end_of, 0)
@@ -337,8 +357,10 @@
     chunk = 512
     early = [h for h in range(heads) if h != middle]
     for h in early:
-        for k in range(1, n_head):
-            a_copy(h, k).wait_recv()
+        for f, k in peers8:
+            a_copy(h, f, k).wait_recv()
+    for copy in b_copies:
+        copy.wait_recv()
 
     def chunk_of(n):
         per_half = half_w // chunk
@@ -347,7 +369,9 @@
 
     def product(h, half, at):
         w = wbuf[half, h, :, :, at].reshape(n_head * HD, chunk)
-        return jnp.dot(arecv[h], w, preferred_element_type=F32)
+        return jnp.dot(
+            arecv[h].reshape(2 * out_rows, n_head * HD), w, preferred_element_type=F32
+        )
 
     def first_heads(n, carry):
         half, at, cols = chunk_of(n)
@@ -358,19 +382,18 @@
         return carry
 
     lax.fori_loop(0, depth // chunk, first_heads, 0)
-    for k in range(1, n_head):
-        a_copy(middle, k).wait_recv()
+    for f, k in peers8:
+        a_copy(middle, f, k).wait_recv()
 
     def last_head(n, carry):
         half, at, cols = chunk_of(n)
         projected = partial[:, cols] + product(middle, half, at)
-        for part in range(2):
-            rows_of = pl.ds(
-                pl.multiple_of(part * n_head * out_rows + x * out_rows, out_rows), out_rows
-            )
-            mixed[pl.ds(part * out_rows, out_rows), cols] = img[rows_of, cols].astype(F32) + mod[
-                2, :, cols
-            ] * projected[part * out_rows : (part + 1) * out_rows]
+        mixed[pl.ds(0, out_rows), cols] = (
+            img[latent_rows(c), cols].astype(F32) + mod[2, :, cols] * projected[:out_rows]
+        )
+        mixed[pl.ds(out_rows, out_rows), cols] = (
+            hid_in[:, cols].astype(F32) + gate_in[:, cols] * projected[out_rows:]
+        )
         values = mixed[:, cols]
         for at in range(0, chunk, HD):
             carry = carry + values[:, at : at + HD]
@@ -387,19 +410,18 @@
     velocity = bfin[...]
     for at in range(0, depth, chunk):
         cols = pl.ds(at, chunk)
-        final_in = ((mixed[:, cols] - mean) * scale * (1.0 + fmod[1:2, cols]) + fmod[0:1, cols]).astype(BF)
+        final_in = (mixed[:, cols] - mean) * scale
+        final_in = jnp.concatenate(
+            [
+                final_in[:out_rows] * (1.0 + fmod[1:2, cols]) + fmod[0:1, cols],
+                final_in[out_rows:] * (1.0 + fmod_in[1:2, cols]) + fmod_in[0:1, cols],
+            ],
+            axis=0,
+        ).astype(BF)
         velocity = velocity + lax.dot_general(
             final_in, wfin[:, cols], (((1,), (1,)), ((), ())), preferred_element_type=F32
         )
     ch = velocity.shape[1]
-    vel[...] = jnp.zeros(vel.shape, F32)
-    vel[0, :, pl.ds(0, ch)] = velocity[:out_rows]
-    vel[1, :, pl.ds(0, ch)] = velocity[out_rows:]
-    swap = pltpu.make_async_remote_copy(
-        src_ref=vel.at[other], dst_ref=vel_in, send_sem=v_send.at[0], recv_sem=v_recv.at[0],
-        device_id={"cfg": other}, device_id_type=MESH,
-    )
-    swap.start()
 
     index = jnp.full((1, ch), step_index[0], jnp.int32).astype(F32)
     count = jnp.full((1, ch), step_count[0], jnp.int32).astype(F32)
@@ -410,9 +432,7 @@
     step_now = log_ratio(sigma_next) - log_ratio(sigma_now)
     step_prev = log_ratio(sigma_now) - log_ratio(sigma_prev)
     ratio = step_prev / step_now
-    swap.wait_recv()
-    ours = vel[c, :, pl.ds(0, ch)]
-    theirs = vel_in[:, pl.ds(0, ch)]
+    ours, theirs = velocity[:out_rows], velocity[out_rows:]
     cond = jnp.where(c == 0, ours, theirs)
     uncond = jnp.where(c == 0, theirs, ours)
     guided = uncond + strength * (cond - uncond)
@@ -439,9 +459,9 @@
         for h, kv in final_pieces[side]:
             hop(side, last, h, kv).wait_send()
     for h in range(heads):
-        for k in range(1, n_head):
-            a_copy(h, k).wait_send()
-    for copy in (w1, w3, w2a, w2b, *d_out, swap):
+        for f, k in peers8:
+            a_copy(h, f, k).wait_send()
+    for copy in (w1, w3, w2a, w2b, *d_out, *b_copies):
         copy.wait_send()
 
 
@@ -498,13 +518,13 @@
             V((heads, 1, rows), F32), V((heads, HD, rows), F32),
             V((last, heads, 2, kv_rows, HD), BF), V((last - 1, heads, 2, kv_rows, HD), BF),
             V((2, heads, n_head, HD, depth // 2), BF),
-            V((heads, n_head, 2 * out_rows, HD), BF), V((heads, 2 * out_rows, n_head * HD), BF),
+            V((heads, 2, n_head, out_rows, HD), BF), V((heads, 2, out_rows, n_head * HD), BF),
             V((2 * out_rows, depth), F32), V((2 * out_rows, depth), F32),
-            V((2, out_rows, 128), F32), V((out_rows, 128), F32),
+            V((out_rows, depth), BF), V((1, depth), F32), V((2, depth), F32),
             dma((heads, 2)), dma((21,)), dma((1,)),
             dma((2, last, heads)), dma((2, last, heads)),
             dma((4,)), dma((4,)), dma((n_head - 1,)), dma((n_head - 1,)),
-            dma((heads, n_head - 1)), dma((heads, n_head - 1)), dma((1,)), dma((1,)),
+            dma((heads, 2, n_head)), dma((heads, 2, n_head)), dma((3,)), dma((3,)),
         ],
         compiler_params=pltpu.CompilerParams(
             collective_id=0, has_side_effects=True, vmem_limit_bytes=60 * 1024 * 1024

time: 113 us -> 112 us (level)
  no operation moved by 1% of the time
where the time goes in v4:
time: 112 us
  Pallas kernels  109 us (97%)
  between operations  2.58 us (2%)
    pallas_call x1, Pallas kernels, body(): pl.pallas_call(functools.partial(kernel, sizes), out_shape=(jax.ShapeDtyp...  107 us

profile of v4, /device:TPU:33, one launch (start us, length us, event | category | flops | bytes accessed | tf_op | source)
XLA Modules:
  0.0 111.7 jit_solution(3162531075967316379)
XLA Ops:
  2.6 107.3 %shard_map.202 = (bf16[2,272,384]{2,1,0:T(8,128)(2,1)}, f32[32,64]{1,0:T(8,128)}, f32[32,64]{1,0:T(8,128)}) custom-call(bf16[256,3072]{1,0:T(8,128)(2,1)} %bitcast.15, bf16[16,3072]{1,0:T(8,128)(2,1)} %bitcast.18, f32[3,1,3072]{2,1,0:T(1,128)} %bitcast.19, bf16[3,3072,384]{2,1,0:T(8,128)(2,1)} %bitcast.13, f32[1,128]{1,0:T(1,128)} %bitcast.22, ...), custom_call_target="tpu_custom_call" | custom-call | tf_op jit(solution)/shard_map/pallas_call | solution.py:501
  109.9 1.8 %shard_map.203 = (bf16[2,272,384]{2,1,0:T(8,128)(2,1)}, f32[32,64]{1,0:T(8,128)}, f32[32,64]{1,0:T(8,128)}) custom-call(bf16[2,272,384]{2,1,0:T(8,128)(2,1)} %get-tuple-element.9.refs_0_, f32[32,64]{1,0:T(8,128)} %get-tuple-element.10.refs_1_, f32[32,64]{1,0:T(8,128)} %get-tuple-element.11.refs_2_), custom_call_target="tpu_custom_call" | custom-call | tf_op jit(solution)/shard_map/pallas_call | solution.py:538
